TPU v7x, 16 devices: a whole 2x2x2 slice. The times are simulated.
16 devices in a mesh: etp: 2 (over z), ep: 8 (over y, x, core).
Axes of the slice: x: 2, y: 2, z: 2, core: 2. Of those that a mesh axis runs over, the one named last changes fastest.
Arguments:
- hidden: bfloat16 [32768, 1024], P(('ep', 'etp'))
- w_router: float32 [1024, 16], replicated
- expert_ids: int32 [32768, 2], P(('ep', 'etp'))
- d_out: bfloat16 [32768, 1024], P(('ep', 'etp'))
- w_gate: bfloat16 [16, 1024, 3584], P('ep', None, 'etp')
- w_up: bfloat16 [16, 1024, 3584], P('ep', None, 'etp')
- w_down: bfloat16 [16, 3584, 1024], P('ep', 'etp')
Outputs:
- output 1: bfloat16 [32768, 1024], P(('ep', 'etp'))
- output 2: bfloat16 [32768, 1024], P(('ep', 'etp'))
- output 3: float32 [1024, 16], replicated
- output 4: float32 [], replicated
- output 5: float32 [16, 1024, 3584], P('ep', None, 'etp')
- output 6: float32 [16, 1024, 3584], P('ep', None, 'etp')
- output 7: float32 [16, 3584, 1024], P('ep', 'etp')
All inputs are finite; a program needn't handle non-finite values.
Results may differ from a plain program's by a relative error of at most 0.00899328.
Values are sent between devices in bfloat16 or wider.
A program may use at most 1 GiB of HBM per device.

v0:
```python
import functools
import jax
import jax.numpy as jnp
from jax import lax
from jax.sharding import PartitionSpec as P

AUX_COEF = 0.01
OUT_SCALE = 2.0


def route_terms(logits, expert_ids):
    prob_vals = jax.nn.softmax(logits, axis=-1)
    picked = jnp.take_along_axis(prob_vals, expert_ids, axis=1)
    return picked / jnp.sum(picked, axis=1, keepdims=True), jnp.sum(prob_vals, axis=0)


def solution(mesh):
    ep_size = mesh.shape["ep"]
    etp_size = mesh.shape["etp"]
    n_dev = ep_size * etp_size
    all_axes = ("ep", "etp")
    tok_spec = P(all_axes, None)
    gate_spec = P("ep", None, "etp")
    down_spec = P("ep", "etp", None)

    def layer(hidden, w_router, expert_ids, d_out, w_gate, w_up, w_down):
        tok_rows, d_model = hidden.shape
        n_experts = w_router.shape[1]
        n_tokens = tok_rows * n_dev
        n_assign = 2 * tok_rows
        capacity = (5 * n_tokens + 2 * n_experts - 1) // (2 * n_experts)
        per_expert = 7 * tok_rows // (2 * n_experts)
        block_idx = lax.axis_index("ep") * etp_size + lax.axis_index("etp")

        hidden_f = hidden.astype(jnp.float32)
        logits = jnp.dot(hidden_f, w_router, preferred_element_type=jnp.float32)
        (gate_vals, prob_sum), route_vjp = jax.vjp(functools.partial(route_terms, expert_ids=expert_ids), logits)

        flat_ids = expert_ids.reshape(-1)
        one_hot = (flat_ids[:, None] == jnp.arange(n_experts, dtype=jnp.int32)[None, :]).astype(jnp.int32)
        local_pos = jnp.sum((jnp.cumsum(one_hot, axis=0) - one_hot) * one_hot, axis=1)
        count_table = lax.all_gather(jnp.sum(one_hot, axis=0), all_axes)
        earlier = (jnp.arange(n_dev) < block_idx)[:, None]
        prefix = jnp.sum(jnp.where(earlier, count_table, 0), axis=0)
        total_count = jnp.sum(count_table, axis=0)
        kept_mask = prefix[flat_ids] + local_pos < capacity
        dest_rows = jnp.where(kept_mask, flat_ids * per_expert + local_pos, n_experts * per_expert)
        source = jnp.full((n_experts * per_expert,), n_assign, jnp.int32).at[dest_rows].set(jnp.arange(n_assign, dtype=jnp.int32), mode="drop")

        def dispatch(values, row_index):
            send_buf = jnp.take(values, row_index, axis=0, mode="fill", fill_value=0).reshape(n_experts, per_expert, d_model)
            received = lax.all_to_all(send_buf, "ep", 0, 1, tiled=True)
            return lax.all_gather(received, "etp", axis=1, tiled=True)

        def combine(part_out):
            summed = lax.psum_scatter(part_out, "etp", scatter_dimension=1, tiled=True).astype(jnp.bfloat16)
            returned = lax.all_to_all(summed, "ep", 1, 0, tiled=True).reshape(n_experts * per_expert, d_model)
            return jnp.take(returned, dest_rows, axis=0, mode="fill", fill_value=0).reshape(tok_rows, 2, d_model)

        x_in = dispatch(hidden, source // 2)
        act_a = jnp.einsum("erd,edf->erf", x_in, w_gate, preferred_element_type=jnp.float32)
        act_b = jnp.einsum("erd,edf->erf", x_in, w_up, preferred_element_type=jnp.float32)
        sig_a = jax.nn.sigmoid(act_a)
        silu_a = act_a * sig_a
        inner_act = (silu_a * act_b).astype(jnp.bfloat16)
        y_pair = combine(jnp.einsum("erf,efd->erd", inner_act, w_down, preferred_element_type=jnp.float32))

        d_mix = OUT_SCALE * d_out.astype(jnp.float32)
        output = (hidden_f + OUT_SCALE * jnp.sum(gate_vals[:, :, None] * y_pair, axis=1)).astype(jnp.bfloat16)
        d_gates = jnp.sum(d_mix[:, None, :] * y_pair, axis=2)
        dy_assign = (gate_vals[:, :, None] * d_mix[:, None, :]).astype(jnp.bfloat16).reshape(n_assign, d_model)
        dy_in = dispatch(dy_assign, source)
        d_inner = jnp.einsum("erd,efd->erf", dy_in, w_down, preferred_element_type=jnp.float32)
        d_act_a = (d_inner * act_b * sig_a * (1.0 + act_a * (1.0 - sig_a))).astype(jnp.bfloat16)
        d_act_b = (d_inner * silu_a).astype(jnp.bfloat16)
        dx_part = jnp.einsum("erf,edf->erd", d_act_a, w_gate, preferred_element_type=jnp.float32) + jnp.einsum("erf,edf->erd", d_act_b, w_up, preferred_element_type=jnp.float32)
        dx_pair = combine(dx_part)
        g_gate = jnp.einsum("erd,erf->edf", x_in, d_act_a, preferred_element_type=jnp.float32)
        g_up = jnp.einsum("erd,erf->edf", x_in, d_act_b, preferred_element_type=jnp.float32)
        g_down = jnp.einsum("erf,erd->efd", inner_act, dy_in, preferred_element_type=jnp.float32)

        route_frac = total_count.astype(jnp.float32) / (2 * n_tokens)
        mean_prob = lax.psum(prob_sum, all_axes) / n_tokens
        aux_loss = AUX_COEF * n_experts * jnp.sum(route_frac * mean_prob)
        (d_logits,) = route_vjp((d_gates, (AUX_COEF * n_experts / n_tokens) * route_frac))
        d_router = lax.psum(jnp.einsum("td,te->de", hidden_f, d_logits, preferred_element_type=jnp.float32), all_axes)
        d_hidden = (d_out.astype(jnp.float32) + jnp.sum(dx_pair, axis=1, dtype=jnp.float32) + jnp.einsum("te,de->td", d_logits, w_router, preferred_element_type=jnp.float32)).astype(jnp.bfloat16)
        return output, d_hidden, d_router, aux_loss, g_gate, g_up, g_down

    return jax.shard_map(layer, mesh=mesh, in_specs=(tok_spec, P(), tok_spec, tok_spec, gate_spec, gate_spec, down_spec), out_specs=(tok_spec, tok_spec, P(), P(), gate_spec, gate_spec, down_spec), check_vma=False)
```

profile of v0, /device:TPU:0, one launch (start us, length us, event | category | flops | bytes accessed | tf_op | source)
XLA Modules:
  0.0 2918.5 jit_solution(12658667043501881361)
XLA Ops:
  17.8 34.7 %all-reduce = s32[256]{0:T(256)S(1)} all-reduce(s32[256]{0:T(256)S(1)} %dynamic-update-slice), channel_id=2, replica_groups=mesh['etp'=2,'ep'=8] {'ep','etp'}, use_global_device_ids=true, to_apply=%add | all-reduce | flops 256 | bytes 2048
  82.4 38.3 %gather_fusion = bf16[7168,1024]{1,0:T(8,128)(2,1)} fusion(bf16[2048,1024]{1,0:T(8,128)(2,1)} %param.9, s32[7168]{0:T(1024)S(1)} %get-tuple-element.35), kind=kCustom, calls=%fused_computation.2 | custom fusion | bytes 29388800 | tf_op jit(solution)/shard_map/jit(_take)/gather | solution.py:51
  128.4 164.7 %all_to_all.66 = bf16[16,448,1024]{2,1,0:T(8,128)(2,1)S(1)} all-to-all(bf16[16,448,1024]{2,1,0:T(8,128)(2,1)S(1)} %broadcast_select_fusion.1), channel_id=1, replica_groups=mesh['etp'=2,'ep'=8] {'ep'}, dimensions={0} | all-to-all | bytes 29360128 | tf_op jit(solution)/shard_map/all_to_all | solution.py:52
  304.8 33.0 %gather_fusion.2 = f32[4096]{0:T(1024)S(1)} fusion(f32[2048,16]{0,1:T(8,128)S(1)} %get-tuple-element.22, s32[4096]{0:T(1024)S(1)} %reshape.264), kind=kCustom, calls=%fused_computation.4 | custom fusion | bytes 65536 | tf_op jit(solution)/shard_map/jvp(jit(take_along_axis))/gather | solution.py:13
  356.7 20.5 mul.147
  386.3 40.0 %gather_fusion.1 = bf16[7168,1024]{1,0:T(8,128)(2,1)} fusion(bf16[4096,1024]{1,0:T(8,128)(2,1)} %multiply_convert_fusion.3, s32[7168]{0:T(1024)S(1)} %copy-done.28), kind=kCustom, calls=%fused_computation.3 | custom fusion | bytes 29388800 | tf_op jit(solution)/shard_map/jit(_take)/gather | solution.py:51
  434.0 164.1 %all_to_all.67 = bf16[16,448,1024]{2,1,0:T(8,128)(2,1)S(1)} all-to-all(bf16[16,448,1024]{2,1,0:T(8,128)(2,1)S(1)} %broadcast_select_fusion), channel_id=1, replica_groups=mesh['etp'=2,'ep'=8] {'ep'}, dimensions={0} | all-to-all | bytes 29360128 | tf_op jit(solution)/shard_map/all_to_all | solution.py:52
  604.3 34.0 %all-gather.4.cloned.1.call-done = bf16[2,7168,1024]{2,1,0:T(8,128)(2,1)} async-done(((bf16[2,3584,1024]{2,1,0:T(8,128)(2,1)}), bf16[2,7168,1024]{2,1,0:T(8,128)(2,1)}) %all-gather.4.cloned.1.call-update) | async-done | bytes 29360144 | tf_op jit(solution)/shard_map/all_gather | solution.py:53
  638.3 63.3 %fusion.21 = f32[2,7168,1792]{2,1,0:T(8,128)} fusion(bf16[2,7168,1024]{2,1,0:T(8,128)(2,1)} %all-gather.4.cloned.1.call-done, bf16[2,1024,1792]{2,1,0:T(8,128)(2,1)} %param.13), kind=kOutput, calls=%fused_computation.103 | convolution fusion | flops 52613349376 | bytes 139460608 | tf_op jit(solution)/shard_map/erd,edf->erf/dot_general | solution.py:61
  701.6 63.3 %fusion.22 = f32[2,7168,1792]{2,1,0:T(8,128)} fusion(bf16[2,7168,1024]{2,1,0:T(8,128)(2,1)} %all-gather.4.cloned.1.call-done, bf16[2,1024,1792]{2,1,0:T(8,128)(2,1)} %param.14), kind=kOutput, calls=%fused_computation.104 | convolution fusion | flops 52613349376 | bytes 139460608 | tf_op jit(solution)/shard_map/erd,edf->erf/dot_general | solution.py:62
  764.9 215.4 %all-gather.6.cloned.1.call-done = bf16[2,7168,1024]{2,1,0:T(8,128)(2,1)} async-done(((bf16[2,3584,1024]{2,1,0:T(8,128)(2,1)}), bf16[2,7168,1024]{2,1,0:T(8,128)(2,1)}) %all-gather.6.cloned.1.call-update) | async-done | bytes 29360144 | tf_op jit(solution)/shard_map/all_gather | solution.py:53
  980.2 148.7 %multiply_convert_fusion = (bf16[2,7168,1792]{2,1,0:T(8,128)(2,1)}, bf16[2,7168,1792]{2,1,0:T(8,128)(2,1)}, bf16[2,7168,1792]{2,1,0:T(8,128)(2,1)}) fusion(f32[2,7168,1792]{2,1,0:T(8,128)} %fusion.21, f32[2,7168,1792]{2,1,0:T(8,128)} %fusion.22, bf16[2,7168,1024]{2,1,0:T(8,128)(2,1)} %all-gather.6.cloned.1.call-done, bf16[2,1792,1024]{2,1,0:T(8,128)(2,1)} %param.15), kind=kOutput, calls=%fused_computation.7 | convolution fusion | flops 52998701056 | bytes 396361728 | tf_op jit(solution)/shard_map/erd,efd->erf/dot_general | solution.py:73
  1129.0 62.9 %fusion.23 = f32[2,7168,1024]{2,1,0:T(8,128)} fusion(bf16[2,7168,1792]{2,1,0:T(8,128)(2,1)} %get-tuple-element.31, bf16[2,1792,1024]{2,1,0:T(8,128)(2,1)} %param.15), kind=kOutput, calls=%fused_computation.105 | convolution fusion | flops 52613349376 | bytes 117440512 | tf_op jit(solution)/shard_map/erf,efd->erd/dot_general | solution.py:66
  1192.0 63.2 %fusion.24 = f32[2,7168,1024]{2,1,0:T(8,128)} fusion(bf16[2,7168,1792]{2,1,0:T(8,128)(2,1)} %get-tuple-element.30, bf16[2,1024,1792]{2,1,0:T(8,128)(2,1)} %param.13), kind=kOutput, calls=%fused_computation.106 | convolution fusion | flops 52613349376 | bytes 117440512 | tf_op jit(solution)/shard_map/erf,edf->erd/dot_general | solution.py:76
  1255.2 68.8 %convolution_add_fusion = f32[2,7168,1024]{2,1,0:T(8,128)} fusion(f32[2,7168,1024]{2,1,0:T(8,128)} %fusion.24, bf16[2,7168,1792]{2,1,0:T(8,128)(2,1)} %get-tuple-element.29, bf16[2,1024,1792]{2,1,0:T(8,128)(2,1)} %param.14), kind=kOutput, calls=%fused_computation.12 | convolution fusion | flops 52628029440 | bytes 176160768 | tf_op jit(solution)/shard_map/erf,edf->erd/dot_general | solution.py:76
  1324.1 505.1 %reduce-scatter.3.cloned.1.call-done = f32[2,3584,1024]{2,1,0:T(8,128)} async-done(((f32[2,7168,1024]{2,1,0:T(8,128)}), f32[2,3584,1024]{2,1,0:T(8,128)}) %reduce-scatter.3.cloned.1.call-update) | async-done | bytes 29360144 | tf_op jit(solution)/shard_map/reduce_scatter | solution.py:56
  1840.0 50.4 %copy.101 = bf16[2,3584,1024]{2,0,1:T(2,128)(2,1)} copy(bf16[2,3584,1024]{2,1,0:T(8,128)(2,1)S(1)} %convert_element_type.62) | data formatting | bytes 29360128 | tf_op jit(solution)/shard_map/convert_element_type | solution.py:56
  1896.2 186.6 %psum.15 = f32[16]{0:T(128)S(1)} all-reduce(f32[16]{0:T(128)S(1)} %copy-done.36), channel_id=1, replica_groups=mesh['etp'=2,'ep'=8] {'ep','etp'}, use_global_device_ids=true, to_apply=%region_20.22 | all-reduce | flops 16 | bytes 128 | tf_op jit(solution)/shard_map/psum | solution.py:83
  2088.5 62.4 %fusion.25 = f32[2,1024,1792]{2,1,0:T(8,128)} fusion(bf16[2,7168,1024]{2,1,0:T(8,128)(2,1)} %all-gather.4.cloned.1.call-done, bf16[2,7168,1792]{2,1,0:T(8,128)(2,1)} %get-tuple-element.30), kind=kOutput, calls=%fused_computation.107 | convolution fusion | flops 52613349376 | bytes 95420416 | tf_op jit(solution)/shard_map/erd,erf->edf/dot_general | solution.py:78
  2150.9 319.1 %reduce-scatter.5.cloned.1.call-done = f32[2,3584,1024]{2,1,0:T(8,128)} async-done(((f32[2,7168,1024]{2,1,0:T(8,128)}), f32[2,3584,1024]{2,1,0:T(8,128)}) %reduce-scatter.5.cloned.1.call-update) | async-done | bytes 29360144 | tf_op jit(solution)/shard_map/reduce_scatter | solution.py:56
  2480.8 50.4 %copy.105 = bf16[2,3584,1024]{2,0,1:T(2,128)(2,1)} copy(bf16[2,3584,1024]{2,1,0:T(8,128)(2,1)S(1)} %convert_element_type.70) | data formatting | bytes 29360128 | tf_op jit(solution)/shard_map/convert_element_type | solution.py:56
  2536.8 62.9 %fusion.26 = f32[2,1024,1792]{2,1,0:T(8,128)} fusion(bf16[2,7168,1024]{2,1,0:T(8,128)(2,1)} %all-gather.4.cloned.1.call-done, bf16[2,7168,1792]{2,1,0:T(8,128)(2,1)} %get-tuple-element.29), kind=kOutput, calls=%fused_computation.108 | convolution fusion | flops 52613349376 | bytes 95420416 | tf_op jit(solution)/shard_map/erd,erf->edf/dot_general | solution.py:79
  2599.7 62.4 %fusion.27 = f32[2,1792,1024]{2,1,0:T(8,128)} fusion(bf16[2,7168,1792]{2,1,0:T(8,128)(2,1)} %get-tuple-element.31, bf16[2,7168,1024]{2,1,0:T(8,128)(2,1)} %all-gather.6.cloned.1.call-done), kind=kOutput, calls=%fused_computation.109 | convolution fusion | flops 52613349376 | bytes 95420416 | tf_op jit(solution)/shard_map/erf,erd->efd/dot_general | solution.py:80
  2677.7 27.9 gather_fusion.3
  2717.3 22.5 scatter_fusion
  2743.5 15.8 copy.106
  2759.3 27.9 gather_fusion.4
  2787.2 16.3 select_convert_fusion
  2803.4 20.0 reshape.208
  2823.5 20.1 reshape.207
  2843.6 25.8 multiply_reduce_fusion.1
  2877.6 23.7 reduce_sum.136
  (170 shorter events, 187.0 us)
Async XLA Ops:
  7.2 293.5 %copy-start = (f32[1024,16]{0,1:T(8,128)S(1)}, f32[1024,16]{0,1:T(8,128)}, u32[]{:S(2)}) copy-start(f32[1024,16]{0,1:T(8,128)} %param.10) | copy-start | bytes 196612
  7.2 631.1 %all-gather.4.cloned.1.call-start = ((), (), s32[]{:S(2)}) async-start(), calls=%async_computation.6 | async-start | bytes 44040192 | tf_op jit(solution)/shard_map/all_gather | solution.py:53
  9.2 111.4 %copy-start.12 = (s32[4096]{0:T(1024)}, s32[4096]{0:T(1024)S(1)}, u32[]{:S(2)}) copy-start(s32[4096]{0:T(1024)S(1)} %eq.25) | copy-start | bytes 49156
  15.6 105.0 %copy-start.14 = (s32[4096]{0:T(1024)}, s32[4096]{0:T(1024)S(1)}, u32[]{:S(2)}) copy-start(s32[4096]{0:T(1024)S(1)} %get-tuple-element.9) | copy-start | bytes 49156
  299.1 681.2 %all-gather.6.cloned.1.call-start = ((), (), s32[]{:S(2)}) async-start(), calls=%async_computation.8 | async-start | bytes 44040192 | tf_op jit(solution)/shard_map/all_gather | solution.py:53
  304.8 34.4 %copy-start.10 = (s32[2048,2]{0,1:T(2,128)S(1)}, s32[2048,2]{0,1:T(2,128)}, u32[]{:S(2)}) copy-start(s32[2048,2]{0,1:T(2,128)} %param.11) | copy-start | bytes 49156
  340.3 16.4 copy-start.3
  356.7 20.5 copy-start.33
  604.1 1225.1 %reduce-scatter.3.cloned.1.call-start = ((), (), s32[]{:S(2)}) async-start(), calls=%async_computation.7 | async-start | bytes 88080384 | tf_op jit(solution)/shard_map/reduce_scatter | solution.py:56
  1191.9 1278.1 %reduce-scatter.5.cloned.1.call-start = ((), (), s32[]{:S(2)}) async-start(), calls=%async_computation.9 | async-start | bytes 88080384 | tf_op jit(solution)/shard_map/reduce_scatter | solution.py:56
  1890.4 192.4 %copy-start.34 = (s32[16]{0:T(128)S(1)}, s32[16]{0:T(128)}, u32[]{:S(2)}) copy-start(s32[16]{0:T(128)} %get-tuple-element.19) | copy-start | bytes 196
  1890.4 193.8 %copy-start.11 = (s32[2048,2]{0,1:T(2,128)S(1)}, s32[2048,2]{0,1:T(2,128)}, u32[]{:S(2)}) copy-start(s32[2048,2]{0,1:T(2,128)} %param.11) | copy-start | bytes 49156
  1890.4 193.9 %copy-start.35 = (s32[2]{0:T(128)S(1)}, s32[2]{0:T(128)}, u32[]{:S(2)}) copy-start(s32[2]{0:T(128)} %constant.119) | copy-start | bytes 28
  1890.4 194.0 %copy-start.37 = (s32[2]{0:T(128)S(1)}, s32[2]{0:T(128)}, u32[]{:S(2)}) copy-start(s32[2]{0:T(128)} %constant.122) | copy-start | bytes 28
  1890.4 196.2 %copy-start.26 = (f32[2048]{0:T(1024)S(1)}, f32[2048]{0:T(1024)}, u32[]{:S(2)}) copy-start(f32[2048]{0:T(1024)} %copy-done.25) | copy-start | bytes 24580
  1890.5 196.8 %copy-start.17 = (f32[2048]{0:T(1024)S(1)}, f32[2048]{0:T(1024)}, u32[]{:S(2)}) copy-start(f32[2048]{0:T(1024)} %copy-done.16) | copy-start | bytes 24580
  1890.5 197.4 %copy-start.13 = (s32[4096]{0:T(1024)S(1)}, s32[4096]{0:T(1024)}, u32[]{:S(2)}) copy-start(s32[4096]{0:T(1024)} %copy-done.12) | copy-start | bytes 49156
  1890.5 197.4 %copy-start.15 = (s32[4096]{0:T(1024)S(1)}, s32[4096]{0:T(1024)}, u32[]{:S(2)}) copy-start(s32[4096]{0:T(1024)} %copy-done.14) | copy-start | bytes 49156
  1890.5 197.4 %copy-start.24 = (s32[4096]{0:T(1024)S(1)}, s32[4096]{0:T(1024)}, u32[]{:S(2)}) copy-start(s32[4096]{0:T(1024)} %copy-done.23) | copy-start | bytes 49156
  1890.5 640.8 %all-to-all-start.1 = ((bf16[2,3584,1024]{2,0,1:T(2,128)(2,1)}), bf16[2,3584,1024]{2,0,1:T(2,128)(2,1)}, u32[]{:S(2)}, u32[]{:S(2)}) async-start(bf16[2,3584,1024]{2,0,1:T(2,128)(2,1)} %copy.101), calls=%async_computation.2 | async-start | bytes 29360128 | tf_op jit(solution)/shard_map/all_to_all | solution.py:57
  2531.3 212.2 %all-to-all-start.3 = ((bf16[2,3584,1024]{2,0,1:T(2,128)(2,1)}), bf16[2,3584,1024]{2,0,1:T(2,128)(2,1)}, u32[]{:S(2)}, u32[]{:S(2)}) async-start(bf16[2,3584,1024]{2,0,1:T(2,128)(2,1)} %copy.105), calls=%async_computation.5 | async-start | bytes 29360128 | tf_op jit(solution)/shard_map/all_to_all | solution.py:57
  2536.8 372.4 %all-reduce.3.cloned.1.call-start = ((), (), s32[]{:S(2)}) async-start(), calls=%async_computation.10 | async-start | bytes 131072 | tf_op jit(solution)/shard_map/psum | solution.py:86
  2662.1 15.6 copy-start.19
  2677.7 27.9 copy-start.29
  2705.6 11.6 copy-start.1
  2717.3 22.6 copy-start.6
  2717.3 22.6 copy-start.8
  2717.3 22.6 copy-start.31
  2717.3 22.6 copy-start.18
  2743.5 15.8 copy-start.20
  2759.3 27.9 copy-start.30
  2823.5 20.1 copy-start.4
  (13 other events, 63.4 us)
Sparse Core Ops, SparseCore 0:
  299.2 339.0 all-gather.3
  640.4 339.7 all-gather.5
  1192.1 637.0 reduce-scatter.2
  1831.3 638.6 reduce-scatter.4
  2743.6 65.2 all-reduce.2
where the time goes:
time: 2930 us; the launch traced here: 2920 us
  waiting for transfers between devices  1070 us (37%)
  matrix products  673 us (23%)
  blocking collectives  550 us (19%)
  local copies, waits for them, and re-layouts  413 us (14%)
  other arithmetic  180 us (6%)
    reduce_scatter x2, waiting for transfers between devices, combine(): lax.psum_scatter(part_out, 'etp', scatter_dimension=1, tiled=True)  824 us
    all_to_all x2, blocking collectives, dispatch(): received = lax.all_to_all(send_buf, 'ep', 0, 1, tiled=True)  329 us
    all_gather x2, waiting for transfers between devices, dispatch(): return lax.all_gather(received, 'etp', axis=1, tiled=True)  249 us
    psum x1, blocking collectives, layer(): mean_prob = lax.psum(prob_sum, all_axes) / n_tokens  187 us
    dot_general x1, matrix products, layer(): jnp.einsum('erd,efd->erf', dy_in, w_down, preferred_element_type=jnp.floa...  149 us
    convert_element_type x2, local copies, waits for them, and re-layouts, combine(): lax.psum_scatter(part_out, 'etp', scatter_dimension=1, tiled=True)  101 us
    gather x2, local copies, waits for them, and re-layouts, dispatch(): jnp.take(values, row_index, axis=0, mode='fill', fill_value=0)  78.3 us
    dot_general x1, matrix products, layer(): jnp.einsum('erf,edf->erd', d_act_b, w_up, preferred_element_type=jnp.floa...  68.8 us
  transfers between devices with their start and end apart: 7, of which 4 were waited for; matrix products, arithmetic and copies ran while one was open for 33% of the time, Pallas kernels for 0%

commit v1 on v0

v1 whole, which is shorter than its diff:
```python
import functools
import jax
import jax.numpy as jnp
from jax import lax
from jax.experimental import pallas as pl
from jax.experimental.pallas import tpu as pltpu
from jax.sharding import PartitionSpec as P

AUX_COEF = 0.01
OUT_SCALE = 2.0
F32 = jnp.float32
BF16 = jnp.bfloat16
SLOT_TILE = 256
TOK_TILE = 256
TOK_BLOCK = 1024
ROW_TILE = 512
COL = 256
VMEM_LIMIT = 62 * 1024 * 1024

NN = (((1,), (0,)), ((), ()))
NT = (((1,), (1,)), ((), ()))


def dot(lhs, rhs, dims=NN):
    return lax.dot_general(lhs, rhs, dims, preferred_element_type=F32)


def params(n_grid):
    return pltpu.CompilerParams(dimension_semantics=("arbitrary",) * n_grid, vmem_limit_bytes=VMEM_LIMIT)


def dispatch_kernel(scaled, n_tiles, start_ref, slot_ref, gate_ref, rows_ref, out_ref):
    block = pl.program_id(0)
    subs = TOK_BLOCK // TOK_TILE

    @pl.when(block == 0)
    def _():
        out_ref[...] = jnp.zeros_like(out_ref)

    slot_iota = lax.broadcasted_iota(jnp.int32, (SLOT_TILE, TOK_TILE), 0)
    for sub in range(subs):
        cols = slice(sub * TOK_TILE, (sub + 1) * TOK_TILE)
        for e in range(2):
            first = start_ref[e, block * subs + sub]
            last = start_ref[e, block * subs + sub + 1]
            for step in range(2):
                tile = lax.shift_right_logical(first, 8) + step

                @pl.when((tile * SLOT_TILE < last) & (tile < n_tiles) & (first < last))
                def _():
                    base = pl.multiple_of(tile * SLOT_TILE, SLOT_TILE)
                    hit = slot_ref[pl.ds(e, 1), cols] == slot_iota + base
                    acc = dot(hit.astype(F32).astype(BF16), rows_ref[cols, :])
                    if scaled:
                        gate = jnp.sum(jnp.where(hit, gate_ref[pl.ds(e, 1), cols], 0.0), axis=1, keepdims=True)
                        acc = acc * (OUT_SCALE * gate)
                    out_ref[e, pl.ds(base, SLOT_TILE), :] += acc.astype(BF16)


def dispatch(scaled, capacity, starts, slots, gates, rows):
    n_tok, d_model = rows.shape
    return pl.pallas_call(
        functools.partial(dispatch_kernel, scaled, capacity // SLOT_TILE),
        out_shape=jax.ShapeDtypeStruct((2, capacity, d_model), BF16),
        grid_spec=pltpu.PrefetchScalarGridSpec(
            num_scalar_prefetch=1,
            grid=(n_tok // TOK_BLOCK,),
            in_specs=[
                pl.BlockSpec((2, TOK_BLOCK), lambda i, s: (0, i)),
                pl.BlockSpec((2, TOK_BLOCK), lambda i, s: (0, i)),
                pl.BlockSpec((TOK_BLOCK, d_model), lambda i, s: (i, 0)),
            ],
            out_specs=pl.BlockSpec((2, capacity, d_model), lambda i, s: (0, 0, 0)),
        ),
        compiler_params=params(1),
        cost_estimate=pl.CostEstimate(flops=40 * 10**9, bytes_accessed=90 * 10**6, transcendentals=0),
        name="dispatch_c" if scaled else "dispatch_x",
    )(starts, slots, gates, rows)


def forward_kernel(pick_ref, x_ref, wg_ref, wu_ref, u_ref, s_ref, t_ref):
    x = x_ref[0]
    for j in range(wg_ref.shape[2] // COL):
        cols = slice(j * COL, (j + 1) * COL)
        a = dot(x, wg_ref[0, :, cols])
        b = dot(x, wu_ref[0, :, cols])
        sig = jax.nn.sigmoid(a)
        silu = a * sig
        u_ref[0, :, cols] = (silu * b).astype(BF16)
        s_ref[0, :, cols] = silu
        t_ref[0, :, cols] = b * sig * (1.0 + a * (1.0 - sig))


def expert_forward(pick, x_in, w_gate, w_up):
    groups, d_model, width = w_gate.shape
    rows = x_in.shape[1]
    out = lambda dt: jax.ShapeDtypeStruct((groups, rows, width), dt)
    wide = pl.BlockSpec((1, ROW_TILE, width), lambda g, m, s: (g, m, 0))
    weight = pl.BlockSpec((1, d_model, width), lambda g, m, s: (g, 0, 0))
    return pl.pallas_call(
        forward_kernel,
        out_shape=(out(BF16), out(F32), out(F32)),
        grid_spec=pltpu.PrefetchScalarGridSpec(
            num_scalar_prefetch=1,
            grid=(groups, rows // ROW_TILE),
            in_specs=[pl.BlockSpec((1, ROW_TILE, d_model), lambda g, m, s: (s[g], m, 0)), weight, weight],
            out_specs=(wide, wide, wide),
        ),
        compiler_params=params(2),
        cost_estimate=pl.CostEstimate(flops=4 * groups * rows * d_model * width, bytes_accessed=groups * rows * width * 12, transcendentals=groups * rows * width),
        name="expert_forward",
    )(pick, x_in, w_gate, w_up)


def backward_kernel(pick_ref, c_ref, wd_ref, s_ref, t_ref, da_ref, db_ref):
    c = c_ref[0]
    for j in range(wd_ref.shape[1] // COL):
        cols = slice(j * COL, (j + 1) * COL)
        du = dot(c, wd_ref[0, cols, :], NT)
        da_ref[0, :, cols] = (du * t_ref[0, :, cols]).astype(BF16)
        db_ref[0, :, cols] = (du * s_ref[0, :, cols]).astype(BF16)


def expert_backward(pick, c_in, w_down, s_act, t_act):
    groups, width, d_model = w_down.shape
    rows = c_in.shape[1]
    out = jax.ShapeDtypeStruct((groups, rows, width), BF16)
    wide = pl.BlockSpec((1, ROW_TILE, width), lambda g, m, s: (g, m, 0))
    return pl.pallas_call(
        backward_kernel,
        out_shape=(out, out),
        grid_spec=pltpu.PrefetchScalarGridSpec(
            num_scalar_prefetch=1,
            grid=(groups, rows // ROW_TILE),
            in_specs=[
                pl.BlockSpec((1, ROW_TILE, d_model), lambda g, m, s: (s[g], m, 0)),
                pl.BlockSpec((1, width, d_model), lambda g, m, s: (g, 0, 0)),
                wide, wide,
            ],
            out_specs=(wide, wide),
        ),
        compiler_params=params(2),
        cost_estimate=pl.CostEstimate(flops=2 * groups * rows * d_model * width, bytes_accessed=groups * rows * width * 12, transcendentals=0),
        name="expert_backward",
    )(pick, c_in, w_down, s_act, t_act)


def project_kernel(dims, n_terms, pick_ref, *refs):
    lhs, rhs, out_ref = refs[:n_terms], refs[n_terms:-1], refs[-1]
    for j in range(out_ref.shape[1] // COL):
        cols = slice(j * COL, (j + 1) * COL)
        total = None
        for left, right in zip(lhs, rhs):
            weight = right[0, cols, :] if dims is NT else right[0, :, cols]
            term = dot(left[0], weight, dims)
            total = term if total is None else total + term
        out_ref[:, cols] = total.astype(BF16)


def project(dims, own, local_acts, other_acts, local_weights, other_weights):
    acts, weights = list(local_acts) + list(other_acts), list(local_weights) + list(other_weights)
    rows, width = acts[0].shape[1:]
    d_model = weights[0].shape[1] if dims is NT else weights[0].shape[2]
    n_local = len(local_acts)
    act_specs = [pl.BlockSpec((1, ROW_TILE, width), (lambda m, s: (s[0], m, 0)) if i < n_local else (lambda m, s: (0, m, 0))) for i in range(len(acts))]
    weight_specs = [pl.BlockSpec((1,) + weights[i].shape[1:], (lambda m, s: (s[0], 0, 0)) if i < n_local else (lambda m, s: (0, 0, 0))) for i in range(len(weights))]
    return pl.pallas_call(
        functools.partial(project_kernel, dims, len(acts)),
        out_shape=jax.ShapeDtypeStruct((rows, d_model), BF16),
        grid_spec=pltpu.PrefetchScalarGridSpec(
            num_scalar_prefetch=1,
            grid=(rows // ROW_TILE,),
            in_specs=act_specs + weight_specs,
            out_specs=pl.BlockSpec((ROW_TILE, d_model), lambda m, s: (m, 0)),
        ),
        compiler_params=params(1),
        cost_estimate=pl.CostEstimate(flops=2 * len(acts) * rows * d_model * width, bytes_accessed=len(acts) * rows * width * 2, transcendentals=0),
    )(own, *acts, *weights)


def window_kernel(start_ref, rows_ref, out_ref):
    start = pl.multiple_of(start_ref[pl.program_id(0)], 16)
    out_ref[0] = rows_ref[pl.ds(start, out_ref.shape[1]), :]


def cut_windows(starts, rows, window):
    n_win, d_model = starts.shape[0], rows.shape[1]
    return pl.pallas_call(
        window_kernel,
        out_shape=jax.ShapeDtypeStruct((n_win, window, d_model), BF16),
        grid_spec=pltpu.PrefetchScalarGridSpec(
            num_scalar_prefetch=1,
            grid=(n_win,),
            in_specs=[pl.BlockSpec(rows.shape, lambda i, s: (0, 0))],
            out_specs=pl.BlockSpec((1, window, d_model), lambda i, s: (i, 0, 0)),
        ),
        compiler_params=params(1),
        cost_estimate=pl.CostEstimate(flops=10**9, bytes_accessed=25 * 10**6, transcendentals=0),
        name="cut_windows",
    )(starts, rows)


def solution(mesh):
    ep_size = mesh.shape["ep"]
    etp_size = mesh.shape["etp"]
    n_dev = ep_size * etp_size
    all_axes = ("ep", "etp")
    tok_spec = P(all_axes, None)
    gate_spec = P("ep", None, "etp")
    down_spec = P("ep", "etp", None)

    def layer_body(hidden, w_router, expert_ids, d_out, w_gate, w_up, w_down):
        tok_rows, d_model = hidden.shape
        n_experts = w_router.shape[1]
        n_tokens = tok_rows * n_dev
        capacity = (5 * n_tokens + 2 * n_experts - 1) // (2 * n_experts)
        per_expert = 7 * tok_rows // (2 * n_experts)
        window = per_expert + 16
        ep_idx, own = lax.axis_index("ep"), lax.axis_index("etp")
        block_idx = ep_idx * etp_size + own

        x_all = lax.all_gather(hidden, all_axes, tiled=True)
        dy_all = lax.all_gather(d_out, all_axes, tiled=True)

        logits = lax.dot_general(w_router, hidden.astype(F32), (((0,), (1,)), ((), ())), preferred_element_type=F32)
        probs = jax.nn.softmax(logits, axis=0)
        ids = expert_ids.T
        expert_iota = lax.broadcasted_iota(jnp.int32, (n_experts, tok_rows), 0)
        hot0, hot1 = expert_iota == ids[0:1], expert_iota == ids[1:2]
        q0 = jnp.sum(jnp.where(hot0, probs, 0.0), axis=0)
        q1 = jnp.sum(jnp.where(hot1, probs, 0.0), axis=0)
        q_sum = q0 + q1
        g0, g1 = q0 / q_sum, q1 / q_sum

        chosen = (hot0 | hot1).astype(F32)
        pad = lambda v: jnp.pad(v, (0, tok_rows - n_experts))
        payload = jnp.stack([ids[0].astype(F32), ids[1].astype(F32), g0, g1, pad(jnp.sum(chosen, axis=1)), pad(jnp.sum(probs, axis=1))])
        gathered = lax.all_gather(payload, all_axes)
        count_table = gathered[:, 4, :n_experts].astype(jnp.int32)
        prob_sum = jnp.sum(gathered[:, 5, :n_experts], axis=0)
        total_count = jnp.sum(count_table, axis=0)
        prefix_table = jnp.cumsum(count_table, axis=0) - count_table
        window_start = jnp.minimum(prefix_table // 16 * 16, capacity - window)

        mine = (2 * ep_idx + jnp.arange(2, dtype=jnp.int32)).astype(F32)[:, None, None]
        id_first, id_second = gathered[None, :, 0], gathered[None, :, 1]
        is_first, is_second = id_first == mine, id_second == mine
        member = (is_first | is_second).reshape(2, n_tokens // 128, 128)
        gate_in = (jnp.where(is_first, gathered[None, :, 2], 0.0) + jnp.where(is_second, gathered[None, :, 3], 0.0)).reshape(2, n_tokens)
        upper = (lax.broadcasted_iota(jnp.int32, (128, 128), 0) <= lax.broadcasted_iota(jnp.int32, (128, 128), 1)).astype(BF16)
        within = lax.dot_general(member.astype(BF16), upper, (((2,), (0,)), ((), ())), preferred_element_type=F32).astype(jnp.int32)
        row_count = within[:, :, 127]
        row_start = jnp.cumsum(row_count, axis=1) - row_count
        slot = row_start[:, :, None] + within - 1
        slots = jnp.where(member & (slot < capacity), slot, -1).reshape(2, n_tokens)
        sub_start = jnp.concatenate([row_start[:, :: TOK_TILE // 128], (row_start + row_count)[:, -1:]], axis=1)

        pick_pair = jnp.arange(2, dtype=jnp.int32)
        pick_own = own.astype(jnp.int32)[None]
        my_windows = lax.dynamic_index_in_dim(window_start, block_idx, 1, keepdims=False)

        x_in = dispatch(False, capacity, sub_start, slots, gate_in, x_all)
        u_near, s_near, t_near = expert_forward(pick_pair, x_in, w_gate, w_up)

        dy_all, wg_sent, wu_sent, wd_sent = lax.optimization_barrier((dy_all, w_gate, w_up, w_down))
        swap = [(0, 1), (1, 0)]
        send_half = lambda w: lax.ppermute(lax.dynamic_slice_in_dim(w, 1 - own, 1, 0), "etp", swap)
        wg_far, wu_far = send_half(wg_sent), send_half(wu_sent)
        wd_far = send_half(wd_sent)

        dy_all, s_near = lax.optimization_barrier((dy_all, s_near))
        c_in = dispatch(True, capacity, sub_start, slots, gate_in, dy_all)
        da_near, db_near = expert_backward(pick_pair, c_in, w_down, s_near, t_near)
        x_again, da_near, db_near = lax.optimization_barrier((x_in, da_near, db_near))

        def windows_of(rows):
            return cut_windows(my_windows, rows, window)

        def give_back(windows):
            return lax.all_to_all(windows, all_axes, 0, 0, tiled=True).reshape(n_experts * window, d_model)

        u_far, s_far, t_far = expert_forward(pick_own, x_again, wg_far, wu_far)
        y_windows = windows_of(project(NN, pick_own, [u_near], [u_far], [w_down], [wd_far]))
        y_windows, s_far = lax.optimization_barrier((y_windows, s_far))
        y_back = give_back(y_windows)
        da_far, db_far = expert_backward(pick_own, c_in, wd_far, s_far, t_far)
        dx_windows = windows_of(project(NT, pick_own, [da_near, db_near], [da_far, db_far], [w_gate, w_up], [wg_far, wu_far]))
        dx_windows, da_near, db_near, u_near = lax.optimization_barrier((dx_windows, da_near, db_near, u_near))
        dx_back = give_back(dx_windows)

        g_gate = jnp.einsum("erd,erf->edf", x_in, da_near, preferred_element_type=F32)
        g_up = jnp.einsum("erd,erf->edf", x_in, db_near, preferred_element_type=F32)
        g_down = jnp.einsum("erf,erd->efd", u_near, c_in, preferred_element_type=F32)

        local_pos = (jnp.cumsum(chosen, axis=1) - chosen).astype(jnp.int32)
        my_prefix = lax.dynamic_index_in_dim(prefix_table, block_idx, 0, keepdims=False)
        my_start = lax.dynamic_index_in_dim(window_start, block_idx, 0, keepdims=False)
        home_slot = my_prefix[:, None] + local_pos
        home_row = jnp.where(home_slot < capacity, expert_iota * window + home_slot - my_start[:, None], -1)
        row0 = jnp.sum(jnp.where(hot0, home_row, 0), axis=0)
        row1 = jnp.sum(jnp.where(hot1, home_row, 0), axis=0)
        pair_rows = jnp.concatenate([row0, row1])

        def pick_rows(back):
            rows = jnp.take(back, jnp.maximum(pair_rows, 0), axis=0, mode="clip")
            rows = jnp.where((pair_rows >= 0)[:, None], rows.astype(F32), 0.0)
            return rows[:tok_rows], rows[tok_rows:]

        hidden_f = hidden.astype(F32)
        dy_f = d_out.astype(F32)
        y0, y1 = pick_rows(y_back)
        output = (hidden_f + OUT_SCALE * (g0[:, None] * y0 + g1[:, None] * y1)).astype(BF16)
        dg0 = jnp.sum(OUT_SCALE * dy_f * y0, axis=1)
        dg1 = jnp.sum(OUT_SCALE * dy_f * y1, axis=1)

        route_frac = total_count.astype(F32) / (2 * n_tokens)
        aux_loss = AUX_COEF * n_experts * jnp.sum(route_frac * prob_sum) / n_tokens
        mixed = dg0 * g0 + dg1 * g1
        dq0, dq1 = (dg0 - mixed) / q_sum, (dg1 - mixed) / q_sum
        d_prob = jnp.where(hot0, dq0[None], 0.0) + jnp.where(hot1, dq1[None], 0.0) + (AUX_COEF * n_experts / n_tokens) * route_frac[:, None]
        d_logits = probs * (d_prob - jnp.sum(probs * d_prob, axis=0, keepdims=True))
        d_router = lax.dot_general(hidden_f, d_logits, (((0,), (1,)), ((), ())), preferred_element_type=F32)
        d_router = lax.psum(d_router, all_axes)
        dx_back, d_logits = lax.optimization_barrier((dx_back, d_logits))
        dx0, dx1 = pick_rows(dx_back)
        d_hidden = (dy_f + (dx0 + dx1) + lax.dot_general(d_logits, w_router, (((0,), (1,)), ((), ())), preferred_element_type=F32)).astype(BF16)
        return output, d_hidden, d_router, aux_loss, g_gate, g_up, g_down

    return jax.shard_map(layer_body, mesh=mesh, in_specs=(tok_spec, P(), tok_spec, tok_spec, gate_spec, gate_spec, down_spec), out_specs=(tok_spec, tok_spec, P(), P(), gate_spec, gate_spec, down_spec), check_vma=False)
```

time: 2930 us -> 1620 us (0.55)
  Pallas kernels: 0 us -> 636 us
  matrix products: 673 us -> 159 us
  blocking collectives: 550 us -> 36.3 us
  waiting for transfers between devices: 1070 us -> 634 us
  local copies, waits for them, and re-layouts: 413 us -> 79.3 us
  other arithmetic: 180 us -> 38.7 us
    reduce_scatter x2 -> x0, waiting for transfers between devices: 824 us -> none  [combine(): lax.psum_scatter(part_out, 'etp', scatter_dimension=1, tiled=True)]
    pallas_call x0 -> x10, Pallas kernels: none -> 636 us  [the longest x2 203 us: dispatch(): pl.pallas_call(functools.partial(dispatch_kernel, scaled, capacity // SLO...]
    dot_general x12 -> x7, matrix products: 673 us -> 159 us  [the longest x1 49.5 us: layer_body(): jnp.einsum('erf,erd->efd', u_near, c_in, preferred_element_type=F32)]
    all_to_all x2 -> x0, blocking collectives: 329 us -> none  [dispatch(): received = lax.all_to_all(send_buf, 'ep', 0, 1, tiled=True)]
    all_gather x2, waiting for transfers between devices: 249 us -> 441 us  [the longest x1 244 us: layer_body(): x_all = lax.all_gather(hidden, all_axes, tiled=True)]
    psum x1 -> x0, blocking collectives: 187 us -> none  [layer(): mean_prob = lax.psum(prob_sum, all_axes) / n_tokens]
    convert_element_type x4 -> x0, local copies, waits for them, and re-layouts: 141 us -> none  [the longest x2 101 us: combine(): lax.psum_scatter(part_out, 'etp', scatter_dimension=1, tiled=True)]
    gather x12 -> x2, local copies, waits for them, and re-layouts: 170 us -> 56.3 us  [pick_rows(): rows = jnp.take(back, jnp.maximum(pair_rows, 0), axis=0, mode='clip')]
  transfers between devices with their start and end apart: 7 -> 8, of which waited for: 4 -> 7; matrix products, arithmetic and copies ran while one was open for 33% -> 14% of each run, Pallas kernels for 0% -> 17%
where the time goes in v1:
time: 1620 us; the launch traced here: 1610 us
  Pallas kernels  636 us (39%)
  waiting for transfers between devices  634 us (39%)
  matrix products  159 us (10%)
  local copies, waits for them, and re-layouts  79.3 us (5%)
  other arithmetic  38.7 us (2%)
  blocking collectives  36.3 us (2%)
  between operations  16.5 us (1%)
    all_gather x1, waiting for transfers between devices, layer_body(): x_all = lax.all_gather(hidden, all_axes, tiled=True)  244 us
    pallas_call x2, Pallas kernels, dispatch(): pl.pallas_call(functools.partial(dispatch_kernel, scaled, capacity // SLO...  203 us
    all_gather x1, waiting for transfers between devices, layer_body(): dy_all = lax.all_gather(d_out, all_axes, tiled=True)  196 us
    pallas_call x2, Pallas kernels, expert_forward(): pl.pallas_call(forward_kernel, out_shape=(out(BF16), out(F32), out(F32)),...  142 us
    pallas_call x2, Pallas kernels, project(): pl.pallas_call(functools.partial(project_kernel, dims, len(acts)), out_sh...  133 us
    pallas_call x2, Pallas kernels, expert_backward(): pl.pallas_call(backward_kernel, out_shape=(out, out), grid_spec=pltpu.Pre...  132 us
    ppermute x3, waiting for transfers between devices, layer_body(): lax.ppermute(lax.dynamic_slice_in_dim(w, 1 - own, 1, 0), 'etp', swap)  90.5 us
    gather x2, local copies, waits for them, and re-layouts, pick_rows(): rows = jnp.take(back, jnp.maximum(pair_rows, 0), axis=0, mode='clip')  56.3 us
  transfers between devices with their start and end apart: 8, of which 7 were waited for; matrix products, arithmetic and copies ran while one was open for 14% of the time, Pallas kernels for 17%

profile of v1, /device:TPU:0, one launch (start us, length us, event | category | flops | bytes accessed | tf_op | source)
XLA Modules:
  0.0 1611.3 jit_solution(17598445308079062973)
XLA Ops:
  13.6 36.3 %all-gather.1 = f32[16,6,2048]{2,1,0:T(8,128)S(1)} all-gather(f32[1,6,2048]{2,1,0:T(8,128)S(1)} %bitcast.87), channel_id=2, replica_groups=mesh['etp'=2,'ep'=8] {'ep','etp'}, dimensions={0}, use_global_device_ids=true | all-gather | bytes 835584 | tf_op jit(solution)/shard_map/all_gather | solution.py:238
  54.2 4.5 reduce-window.14
  64.7 196.4 %all-gather.7.cloned.1.call-done.rows_ref = bf16[32768,1024]{1,0:T(8,128)(2,1)} async-done(((bf16[2048,1024]{1,0:T(8,128)(2,1)}), bf16[32768,1024]{1,0:T(8,128)(2,1)}) %all-gather.7.cloned.1.call-update) | async-done | bytes 67108880 | tf_op jit(solution)/shard_map/all_gather | solution.py:223
  261.1 244.3 %all-gather.5.cloned.1.call-done.rows_ref = bf16[32768,1024]{1,0:T(8,128)(2,1)} async-done(((bf16[2048,1024]{1,0:T(8,128)(2,1)}), bf16[32768,1024]{1,0:T(8,128)(2,1)}) %all-gather.5.cloned.1.call-update) | async-done | bytes 67108880 | tf_op jit(solution)/shard_map/all_gather | solution.py:222
  505.4 100.2 %dispatch_x.1.x_ref = bf16[2,5120,1024]{2,1,0:T(8,128)(2,1)} custom-call(s32[2,129]{1,0:T(2,128)} %pad_add_fusion.start_ref, s32[2,32768]{1,0:T(2,128)} %bitcast.88, f32[2,32768]{1,0:T(2,128)} %fusion.6.gate_ref, bf16[32768,1024]{1,0:T(8,128)(2,1)} %all-gather.5.cloned.1.call-done.rows_ref), custom_call_target="tpu_custom_call" | custom-call | flops 40000000000 | bytes 90000000 | tf_op jit(solution)/shard_map/dispatch_x/pallas_call | solution.py:62
  606.2 94.2 %expert_forward.2 = (bf16[2,5120,1792]{2,1,0:T(8,128)(2,1)}, f32[2,5120,1792]{2,1,0:T(8,128)}, f32[2,5120,1792]{2,1,0:T(8,128)}) custom-call(s32[2]{0:T(128)} %iota.65.pick_ref, bf16[2,5120,1024]{2,1,0:T(8,128)(2,1)} %dispatch_x.1.x_ref, bf16[2,1024,1792]{2,1,0:T(8,128)(2,1)} %refs_4_.1, bf16[2,1024,1792]{2,1,0:T(8,128)(2,1)} %refs_5_.1), custom_call_target="tpu_custom_call" | custom-call | flops 75161927680 | bytes 220200960 | tf_op jit(solution)/shard_map/expert_forward/pallas_call | solution.py:100
  700.4 103.3 %dispatch_c.1.c_ref = bf16[2,5120,1024]{2,1,0:T(8,128)(2,1)} custom-call(s32[2,129]{1,0:T(2,128)} %pad_add_fusion.start_ref, s32[2,32768]{1,0:T(2,128)} %bitcast.89, f32[2,32768]{1,0:T(2,128)} %fusion.6.gate_ref, bf16[32768,1024]{1,0:T(8,128)(2,1)} %all-gather.7.cloned.1.call-done.rows_ref), custom_call_target="tpu_custom_call" | custom-call | flops 40000000000 | bytes 90000000 | tf_op jit(solution)/shard_map/dispatch_c/pallas_call | solution.py:62
  803.7 4.3 constant_dynamic-slice_fusion.2
  812.1 4.2 constant_dynamic-slice_fusion
  818.0 86.7 %expert_backward.2 = (bf16[2,5120,1792]{2,1,0:T(8,128)(2,1)}, bf16[2,5120,1792]{2,1,0:T(8,128)(2,1)}) custom-call(s32[2]{0:T(128)} %iota.69.pick_ref, bf16[2,5120,1024]{2,1,0:T(8,128)(2,1)} %dispatch_c.1.c_ref, bf16[2,1792,1024]{2,1,0:T(8,128)(2,1)} %refs_2_.1, f32[2,5120,1792]{2,1,0:T(8,128)} %get-tuple-element.38.s_ref, ...), custom_call_target="tpu_custom_call" | custom-call | flops 37580963840 | bytes 220200960 | tf_op jit(solution)/shard_map/expert_backward/pallas_call | solution.py:129
  904.7 64.5 %collective-permute-done.1.wu_ref.refs_7_ = bf16[1,1024,1792]{2,1,0:T(8,128)(2,1)} collective-permute-done((bf16[1,1024,1792]{2,1,0:T(8,128)(2,1)}, bf16[1,1024,1792]{2,1,0:T(8,128)(2,1)}, u32[]{:S(2)}, u32[]{:S(2)}) %collective-permute-start.1) | collective-permute-done | bytes 3670048 | tf_op jit(solution)/shard_map/ppermute | solution.py:267
  969.2 47.6 %expert_forward.3 = (bf16[1,5120,1792]{2,1,0:T(8,128)(2,1)}, f32[1,5120,1792]{2,1,0:T(8,128)}, f32[1,5120,1792]{2,1,0:T(8,128)}) custom-call(s32[1]{0:T(128)} %bitcast.15.pick_ref, bf16[2,5120,1024]{2,1,0:T(8,128)(2,1)} %dispatch_x.1.x_ref, bf16[1,1024,1792]{2,1,0:T(8,128)(2,1)} %collective-permute-done.wg_ref.refs_6_, ...), custom_call_target="tpu_custom_call" | custom-call | flops 37580963840 | bytes 110100480 | tf_op jit(solution)/shard_map/expert_forward/pallas_call | solution.py:100
  1016.8 26.0 %collective-permute-done.2.refs_3_.wd_ref = bf16[1,1792,1024]{2,1,0:T(8,128)(2,1)} collective-permute-done((bf16[1,1792,1024]{2,1,0:T(8,128)(2,1)}, bf16[1,1792,1024]{2,1,0:T(8,128)(2,1)}, u32[]{:S(2)}, u32[]{:S(2)}) %collective-permute-start.2) | collective-permute-done | bytes 3670048 | tf_op jit(solution)/shard_map/ppermute | solution.py:267
  1042.8 45.3 %shard_map.126.rows_ref = bf16[5120,1024]{1,0:T(8,128)(2,1)} custom-call(s32[1]{0:T(128)} %bitcast.15.pick_ref, bf16[2,5120,1792]{2,1,0:T(8,128)(2,1)} %get-tuple-element.60.refs_0_, bf16[1,5120,1792]{2,1,0:T(8,128)(2,1)} %get-tuple-element.45.refs_1_, bf16[2,1792,1024]{2,1,0:T(8,128)(2,1)} %refs_2_.1, ...), custom_call_target="tpu_custom_call" | custom-call | flops 37580963840 | bytes 36700160 | tf_op jit(solution)/shard_map/pallas_call | solution.py:167
  1088.1 13.1 cut_windows.2
  1101.2 4.7 all-to-all-start
  1106.0 45.0 %expert_backward.3 = (bf16[1,5120,1792]{2,1,0:T(8,128)(2,1)}, bf16[1,5120,1792]{2,1,0:T(8,128)(2,1)}) custom-call(s32[1]{0:T(128)} %bitcast.15.pick_ref, bf16[2,5120,1024]{2,1,0:T(8,128)(2,1)} %dispatch_c.1.c_ref, bf16[1,1792,1024]{2,1,0:T(8,128)(2,1)} %collective-permute-done.2.refs_3_.wd_ref, f32[1,5120,1792]{2,1,0:T(8,128)} %get-tuple-element.51.s_ref, ...), custom_call_target="tpu_custom_call" | custom-call | flops 18790481920 | bytes 110100480 | tf_op jit(solution)/shard_map/expert_backward/pallas_call | solution.py:129
  1151.0 87.3 %shard_map.127.rows_ref = bf16[5120,1024]{1,0:T(8,128)(2,1)} custom-call(s32[1]{0:T(128)} %bitcast.15.pick_ref, bf16[2,5120,1792]{2,1,0:T(8,128)(2,1)} %get-tuple-element.58.refs_0_, bf16[2,5120,1792]{2,1,0:T(8,128)(2,1)} %get-tuple-element.59.refs_1_, bf16[1,5120,1792]{2,1,0:T(8,128)(2,1)} %get-tuple-element.53.refs_2_, ...), custom_call_target="tpu_custom_call" | custom-call | flops 75161927680 | bytes 73400320 | tf_op jit(solution)/shard_map/pallas_call | solution.py:167
  1238.3 13.1 cut_windows.3
  1251.4 47.5 %fusion.28 = f32[2,1024,1792]{2,1,0:T(8,128)} fusion(bf16[2,5120,1024]{2,1,0:T(8,128)(2,1)} %dispatch_x.1.x_ref, bf16[2,5120,1792]{2,1,0:T(8,128)(2,1)} %get-tuple-element.58.refs_0_), kind=kOutput, calls=%fused_computation.92 | convolution fusion | flops 37580963840 | bytes 72351744 | tf_op jit(solution)/shard_map/erd,erf->edf/dot_general | solution.py:291
  1300.4 4.5 all-to-all-start.1
  1305.0 47.5 %fusion.29 = f32[2,1024,1792]{2,1,0:T(8,128)} fusion(bf16[2,5120,1024]{2,1,0:T(8,128)(2,1)} %dispatch_x.1.x_ref, bf16[2,5120,1792]{2,1,0:T(8,128)(2,1)} %get-tuple-element.59.refs_1_), kind=kOutput, calls=%fused_computation.93 | convolution fusion | flops 37580963840 | bytes 72351744 | tf_op jit(solution)/shard_map/erd,erf->edf/dot_general | solution.py:292
  1352.6 49.5 %fusion.30 = f32[2,1792,1024]{2,1,0:T(8,128)} fusion(bf16[2,5120,1792]{2,1,0:T(8,128)(2,1)} %get-tuple-element.60.refs_0_, bf16[2,5120,1024]{2,1,0:T(8,128)(2,1)} %dispatch_c.1.c_ref), kind=kOutput, calls=%fused_computation.94 | convolution fusion | flops 37580963840 | bytes 72351744 | tf_op jit(solution)/shard_map/erf,erd->efd/dot_general | solution.py:293
  1402.0 28.1 %gather_fusion = bf16[4096,1024]{1,0:T(8,128)(2,1)} fusion(bf16[7424,1024]{1,0:T(8,128)(2,1)} %bitcast.25, s32[4096]{0:T(1024)S(1)} %copy-done.13), kind=kCustom, calls=%fused_computation | custom fusion | bytes 16793600 | tf_op jit(solution)/shard_map/jit(_take)/gather | solution.py:305
  1430.2 5.0 convert_select_fusion.1
  1437.7 4.8 copy-done.1
  1444.1 10.4 add_convert_fusion
  1454.4 44.1 %all-to-all-done.1 = bf16[16,464,1024]{2,1,0:T(8,128)(2,1)} async-done(((bf16[16,464,1024]{2,1,0:T(8,128)(2,1)}), bf16[16,464,1024]{2,1,0:T(8,128)(2,1)}, u32[]{:S(2)}, u32[]{:S(2)}) %all-to-all-start.1) | async-done | bytes 15204384 | tf_op jit(solution)/shard_map/all_to_all | solution.py:280
  1498.5 28.2 %gather_fusion.1 = bf16[4096,1024]{1,0:T(8,128)(2,1)} fusion(bf16[7424,1024]{1,0:T(8,128)(2,1)} %bitcast.29, s32[4096]{0:T(1024)S(1)} %copy-done.13), kind=kCustom, calls=%fused_computation.1 | custom fusion | bytes 16793600 | tf_op jit(solution)/shard_map/jit(_take)/gather | solution.py:305
  1526.7 9.7 convert_select_fusion
  1536.4 9.9 fusion.5
  1546.3 55.4 %all-reduce.4.cloned.1.call-done = f32[1024,16]{0,1:T(8,128)} async-done(((f32[1024,16]{0,1:T(8,128)}), f32[1024,16]{0,1:T(8,128)}) %all-reduce.4.cloned.1.call-update) | async-done | bytes 65552 | tf_op jit(solution)/shard_map/psum | solution.py:323
  (115 shorter events, 29.2 us)
Async XLA Ops:
  7.2 1.5 copy-start
  7.2 5.0 copy-start.21
  7.2 253.9 %all-gather.7.cloned.1.call-start = ((), (), s32[]{:S(2)}) async-start(), calls=%async_computation.3 | async-start | bytes 71303168 | tf_op jit(solution)/shard_map/all_gather | solution.py:223
  7.9 497.5 %all-gather.5.cloned.1.call-start = ((), (), s32[]{:S(2)}) async-start(), calls=%async_computation.2 | async-start | bytes 71303168 | tf_op jit(solution)/shard_map/all_gather | solution.py:222
  12.1 0.6 copy-start.4
  12.1 0.9 copy-start.11
  12.2 0.8 copy-start.14
  12.2 593.4 %copy-start.7 = (s32[1,2048]{1,0:T(1,128)}, s32[1,2048]{1,0:T(1,128)S(1)}, u32[]{:S(2)}) copy-start(s32[1,2048]{1,0:T(1,128)S(1)} %get-tuple-element.83) | copy-start | bytes 24580
  12.2 593.4 %copy-start.9 = (s32[1,2048]{1,0:T(1,128)}, s32[1,2048]{1,0:T(1,128)S(1)}, u32[]{:S(2)}) copy-start(s32[1,2048]{1,0:T(1,128)S(1)} %get-tuple-element.86) | copy-start | bytes 24580
  13.0 0.6 copy-start.16
  13.0 0.6 copy-start.18
  803.7 5.5 copy-start.6
  808.0 96.7 %collective-permute-start = (bf16[1,1024,1792]{2,1,0:T(8,128)(2,1)}, bf16[1,1024,1792]{2,1,0:T(8,128)(2,1)}, u32[]{:S(2)}, u32[]{:S(2)}) collective-permute-start(bf16[1,1024,1792]{2,1,0:T(8,128)(2,1)} %constant_dynamic-slice_fusion.2), channel_id=1, source_target_pairs={{0,8},{8,0},{1,9},{9,1},{2,10},{10,2},{3,11},{11,3},{4,12},{12,4},... | collective-permute-start | bytes 11010056 | tf_op jit(solution)/shard_map/ppermute | solution.py:267
  811.3 157.9 %collective-permute-start.1 = (bf16[1,1024,1792]{2,1,0:T(8,128)(2,1)}, bf16[1,1024,1792]{2,1,0:T(8,128)(2,1)}, u32[]{:S(2)}, u32[]{:S(2)}) collective-permute-start(bf16[1,1024,1792]{2,1,0:T(8,128)(2,1)} %constant_dynamic-slice_fusion.1), channel_id=1, source_target_pairs={{0,8},{8,0},{1,9},{9,1},{2,10},{10,2},{3,11},{11,3},{4,12},{12,4},... | collective-permute-start | bytes 11010056 | tf_op jit(solution)/shard_map/ppermute | solution.py:267
  816.3 226.4 %collective-permute-start.2 = (bf16[1,1792,1024]{2,1,0:T(8,128)(2,1)}, bf16[1,1792,1024]{2,1,0:T(8,128)(2,1)}, u32[]{:S(2)}, u32[]{:S(2)}) collective-permute-start(bf16[1,1792,1024]{2,1,0:T(8,128)(2,1)} %constant_dynamic-slice_fusion), channel_id=1, source_target_pairs={{0,8},{8,0},{1,9},{9,1},{2,10},{10,2},{3,11},{11,3},{4,12},{12,4},... | collective-permute-start | bytes 11010056 | tf_op jit(solution)/shard_map/ppermute | solution.py:267
  1101.2 199.2 %all-to-all-start = ((bf16[16,464,1024]{2,1,0:T(8,128)(2,1)}), bf16[16,464,1024]{2,1,0:T(8,128)(2,1)}, u32[]{:S(2)}, u32[]{:S(2)}) async-start(bf16[16,464,1024]{2,1,0:T(8,128)(2,1)} %cut_windows.2), calls=%async_computation | async-start | bytes 30408704 | tf_op jit(solution)/shard_map/all_to_all | solution.py:280
  1300.4 198.1 %all-to-all-start.1 = ((bf16[16,464,1024]{2,1,0:T(8,128)(2,1)}), bf16[16,464,1024]{2,1,0:T(8,128)(2,1)}, u32[]{:S(2)}, u32[]{:S(2)}) async-start(bf16[16,464,1024]{2,1,0:T(8,128)(2,1)} %cut_windows.3), calls=%async_computation.1 | async-start | bytes 30408704 | tf_op jit(solution)/shard_map/all_to_all | solution.py:280
  1305.0 296.7 %all-reduce.4.cloned.1.call-start = ((), (), s32[]{:S(2)}) async-start(), calls=%async_computation.4 | async-start | bytes 131072 | tf_op jit(solution)/shard_map/psum | solution.py:323
  1352.6 49.5 %copy-start.13 = (s32[4096]{0:T(1024)S(1)}, s32[4096]{0:T(1024)}, u32[]{:S(2)}) copy-start(s32[4096]{0:T(1024)} %broadcast_clamp_fusion) | copy-start | bytes 49156
  1402.0 28.2 %copy-start.20 = (pred[4096]{0:T(1024)(128)(4,1)S(1)}, pred[4096]{0:T(1024)(128)(4,1)}, u32[]{:S(2)}) copy-start(pred[4096]{0:T(1024)(128)(4,1)} %add_compare_fusion) | copy-start | bytes 12292
  1430.2 5.0 copy-start.3
  1435.2 7.3 copy-start.1
  1435.2 7.3 copy-start.17
  1435.2 7.3 copy-start.19
  1435.2 7.3 copy-start.5
  1435.2 7.3 copy-start.8
  1435.3 7.3 copy-start.10
  1435.3 7.3 copy-start.12
  1435.3 7.3 copy-start.15
  1435.3 7.3 copy-start.22
  1435.3 7.5 copy-start.2
Sparse Core Ops, SparseCore 0:
  10.2 250.8 all-gather.6
  263.3 242.0 all-gather.4
  1536.5 65.1 all-reduce.3

commit v2 on v1

--- a/solution.py
+++ b/solution.py
@@ -11,11 +11,13 @@
 F32 = jnp.float32
 BF16 = jnp.bfloat16
 SLOT_TILE = 256
-TOK_TILE = 256
+TOK_TILE = 512
 TOK_BLOCK = 1024
 ROW_TILE = 512
 COL = 256
 VMEM_LIMIT = 62 * 1024 * 1024
+
+SEND_ORDER = (13, 9, 1, 15, 11, 3, 12, 8, 14, 10, 5, 7, 4, 6, 2)
 
 NN = (((1,), (0,)), ((), ()))
 NT = (((1,), (1,)), ((), ()))
@@ -43,7 +45,7 @@
         for e in range(2):
             first = start_ref[e, block * subs + sub]
             last = start_ref[e, block * subs + sub + 1]
-            for step in range(2):
+            for step in range(TOK_TILE // SLOT_TILE + 1):
                 tile = lax.shift_right_logical(first, 8) + step
 
                 @pl.when((tile * SLOT_TILE < last) & (tile < n_tiles) & (first < last))
@@ -178,26 +180,48 @@
     )(own, *acts, *weights)
 
 
-def window_kernel(start_ref, rows_ref, out_ref):
-    start = pl.multiple_of(start_ref[pl.program_id(0)], 16)
-    out_ref[0] = rows_ref[pl.ds(start, out_ref.shape[1]), :]
+def window_kernel(start_ref, rows_ref, *out_refs):
+    for i, out_ref in enumerate(out_refs):
+        start = pl.multiple_of(start_ref[i], 16)
+        out_ref[...] = rows_ref[pl.ds(start, out_ref.shape[0]), :]
 
 
 def cut_windows(starts, rows, window):
-    n_win, d_model = starts.shape[0], rows.shape[1]
+    n_win, (n_rows, d_model) = starts.shape[0], rows.shape
     return pl.pallas_call(
         window_kernel,
-        out_shape=jax.ShapeDtypeStruct((n_win, window, d_model), BF16),
-        grid_spec=pltpu.PrefetchScalarGridSpec(
-            num_scalar_prefetch=1,
-            grid=(n_win,),
-            in_specs=[pl.BlockSpec(rows.shape, lambda i, s: (0, 0))],
-            out_specs=pl.BlockSpec((1, window, d_model), lambda i, s: (i, 0, 0)),
+        out_shape=(jax.ShapeDtypeStruct((window, d_model), BF16),) * n_win,
+        grid_spec=pltpu.PrefetchScalarGridSpec(
+            num_scalar_prefetch=1,
+            grid=(d_model // COL,),
+            in_specs=[pl.BlockSpec((n_rows, COL), lambda i, s: (0, i))],
+            out_specs=(pl.BlockSpec((window, COL), lambda i, s: (0, i)),) * n_win,
         ),
         compiler_params=params(1),
         cost_estimate=pl.CostEstimate(flops=10**9, bytes_accessed=25 * 10**6, transcendentals=0),
         name="cut_windows",
     )(starts, rows)
+
+
+def join_kernel(*refs):
+    blocks, out_ref = refs[:-1], refs[-1]
+    window = blocks[0].shape[0]
+    for i, block in enumerate(blocks):
+        out_ref[i * window : (i + 1) * window, :] = block[...]
+
+
+def join_windows(blocks):
+    n_win, (window, d_model) = len(blocks), blocks[0].shape
+    return pl.pallas_call(
+        join_kernel,
+        out_shape=jax.ShapeDtypeStruct((n_win * window, d_model), BF16),
+        grid=(d_model // COL,),
+        in_specs=[pl.BlockSpec((window, COL), lambda i: (0, i))] * n_win,
+        out_specs=pl.BlockSpec((n_win * window, COL), lambda i: (0, i)),
+        compiler_params=params(1),
+        cost_estimate=pl.CostEstimate(flops=10**9, bytes_accessed=30 * 10**6, transcendentals=0),
+        name="join_windows",
+    )(*blocks)
 
 
 def solution(mesh):
@@ -210,7 +234,7 @@
     down_spec = P("ep", "etp", None)
 
     def layer_body(hidden, w_router, expert_ids, d_out, w_gate, w_up, w_down):
-        tok_rows, d_model = hidden.shape
+        tok_rows, _ = hidden.shape
         n_experts = w_router.shape[1]
         n_tokens = tok_rows * n_dev
         capacity = (5 * n_tokens + 2 * n_experts - 1) // (2 * n_experts)
@@ -257,14 +281,17 @@
 
         pick_pair = jnp.arange(2, dtype=jnp.int32)
         pick_own = own.astype(jnp.int32)[None]
-        my_windows = lax.dynamic_index_in_dim(window_start, block_idx, 1, keepdims=False)
+        partner = jnp.arange(n_dev, dtype=jnp.int32) ^ block_idx
+        my_windows = jnp.take(lax.dynamic_index_in_dim(window_start, block_idx, 1, keepdims=False), partner)
 
         x_in = dispatch(False, capacity, sub_start, slots, gate_in, x_all)
         u_near, s_near, t_near = expert_forward(pick_pair, x_in, w_gate, w_up)
 
-        dy_all, wg_sent, wu_sent, wd_sent = lax.optimization_barrier((dy_all, w_gate, w_up, w_down))
+        half_of = lambda w: lax.dynamic_slice_in_dim(w, 1 - own, 1, 0)
+        wg_sent, wu_sent, wd_sent = lax.optimization_barrier((half_of(w_gate), half_of(w_up), half_of(w_down)))
+        dy_all, wg_sent, wu_sent, wd_sent = lax.optimization_barrier((dy_all, wg_sent, wu_sent, wd_sent))
         swap = [(0, 1), (1, 0)]
-        send_half = lambda w: lax.ppermute(lax.dynamic_slice_in_dim(w, 1 - own, 1, 0), "etp", swap)
+        send_half = lambda w: lax.ppermute(w, "etp", swap)
         wg_far, wu_far = send_half(wg_sent), send_half(wu_sent)
         wd_far = send_half(wd_sent)
 
@@ -277,26 +304,30 @@
             return cut_windows(my_windows, rows, window)
 
         def give_back(windows):
-            return lax.all_to_all(windows, all_axes, 0, 0, tiled=True).reshape(n_experts * window, d_model)
+            place = lambda b: (b % etp_size) * ep_size + b // etp_size
+            blocks = list(windows)
+            for i in SEND_ORDER:
+                blocks[i] = lax.ppermute(windows[i], ("etp", "ep"), [(place(b), place(b ^ i)) for b in range(n_dev)])
+            return blocks
 
         u_far, s_far, t_far = expert_forward(pick_own, x_again, wg_far, wu_far)
         y_windows = windows_of(project(NN, pick_own, [u_near], [u_far], [w_down], [wd_far]))
         y_windows, s_far = lax.optimization_barrier((y_windows, s_far))
-        y_back = give_back(y_windows)
+        y_blocks = give_back(y_windows)
+        y_back = join_windows(y_blocks)
         da_far, db_far = expert_backward(pick_own, c_in, wd_far, s_far, t_far)
         dx_windows = windows_of(project(NT, pick_own, [da_near, db_near], [da_far, db_far], [w_gate, w_up], [wg_far, wu_far]))
         dx_windows, da_near, db_near, u_near = lax.optimization_barrier((dx_windows, da_near, db_near, u_near))
-        dx_back = give_back(dx_windows)
+        dx_blocks = give_back(dx_windows)
+        dx_back = join_windows(dx_blocks)
 
         g_gate = jnp.einsum("erd,erf->edf", x_in, da_near, preferred_element_type=F32)
         g_up = jnp.einsum("erd,erf->edf", x_in, db_near, preferred_element_type=F32)
-        g_down = jnp.einsum("erf,erd->efd", u_near, c_in, preferred_element_type=F32)
-
         local_pos = (jnp.cumsum(chosen, axis=1) - chosen).astype(jnp.int32)
         my_prefix = lax.dynamic_index_in_dim(prefix_table, block_idx, 0, keepdims=False)
         my_start = lax.dynamic_index_in_dim(window_start, block_idx, 0, keepdims=False)
         home_slot = my_prefix[:, None] + local_pos
-        home_row = jnp.where(home_slot < capacity, expert_iota * window + home_slot - my_start[:, None], -1)
+        home_row = jnp.where(home_slot < capacity, (expert_iota ^ block_idx) * window + home_slot - my_start[:, None], -1)
         row0 = jnp.sum(jnp.where(hot0, home_row, 0), axis=0)
         row1 = jnp.sum(jnp.where(hot1, home_row, 0), axis=0)
         pair_rows = jnp.concatenate([row0, row1])
@@ -320,7 +351,9 @@
         d_prob = jnp.where(hot0, dq0[None], 0.0) + jnp.where(hot1, dq1[None], 0.0) + (AUX_COEF * n_experts / n_tokens) * route_frac[:, None]
         d_logits = probs * (d_prob - jnp.sum(probs * d_prob, axis=0, keepdims=True))
         d_router = lax.dot_general(hidden_f, d_logits, (((0,), (1,)), ((), ())), preferred_element_type=F32)
+        u_near, d_router = lax.optimization_barrier((u_near, d_router))
         d_router = lax.psum(d_router, all_axes)
+        g_down = jnp.einsum("erf,erd->efd", u_near, c_in, preferred_element_type=F32)
         dx_back, d_logits = lax.optimization_barrier((dx_back, d_logits))
         dx0, dx1 = pick_rows(dx_back)
         d_hidden = (dy_f + (dx0 + dx1) + lax.dot_general(d_logits, w_router, (((0,), (1,)), ((), ())), preferred_element_type=F32)).astype(BF16)

time: 1620 us -> 1920 us (1.19)
  waiting for transfers between devices: 634 us -> 943 us
  starting transfers between devices: 11.8 us -> 35.2 us
    all_gather x1, waiting for transfers between devices: 244 us -> 452 us  [layer_body(): x_all = lax.all_gather(hidden, all_axes, tiled=True)]
    ppermute x3 -> x33, waiting for transfers between devices: 90.5 us -> 253 us  [the longest x30 253 us: give_back(): lax.ppermute(windows[i], ('etp', 'ep'), [(place(b), place(b ^ i)) for b i...]
    all_to_all x2 -> x0, waiting for transfers between devices: 45.7 us -> none  [give_back(): lax.all_to_all(windows, all_axes, 0, 0, tiled=True)]
    pallas_call x2, Pallas kernels: 203 us -> 170 us  [dispatch(): pl.pallas_call(functools.partial(dispatch_kernel, scaled, capacity // SLO...]
    ppermute x3 -> x33, starting transfers between devices: 2.38 us -> 35.1 us  [the longest x30 32.8 us: give_back(): lax.ppermute(windows[i], ('etp', 'ep'), [(place(b), place(b ^ i)) for b i...]
    pallas_call x2 -> x4, Pallas kernels: 26.2 us -> 42.5 us  [the longest x2 22 us: join_windows(): pl.pallas_call(join_kernel, out_shape=jax.ShapeDtypeStruct((n_win * windo...]
  transfers between devices with their start and end apart: 8 -> 36, of which waited for: 7 -> 12; matrix products, arithmetic and copies ran while one was open for 14% -> 9% of each run, Pallas kernels for 17% -> 29%
where the time goes in v2:
time: 1920 us
  waiting for transfers between devices  943 us (49%)
  Pallas kernels  618 us (32%)
  matrix products  153 us (8%)
  local copies, waits for them, and re-layouts  81.2 us (4%)
  blocking collectives  37.1 us (2%)
  starting transfers between devices  35.2 us (2%)
  other arithmetic  34.7 us (2%)
    all_gather x1, waiting for transfers between devices, layer_body(): x_all = lax.all_gather(hidden, all_axes, tiled=True)  452 us
    ppermute x30, waiting for transfers between devices, give_back(): lax.ppermute(windows[i], ('etp', 'ep'), [(place(b), place(b ^ i)) for b i...  253 us
    all_gather x1, waiting for transfers between devices, layer_body(): dy_all = lax.all_gather(d_out, all_axes, tiled=True)  183 us
    pallas_call x2, Pallas kernels, dispatch(): pl.pallas_call(functools.partial(dispatch_kernel, scaled, capacity // SLO...  170 us
    pallas_call x2, Pallas kernels, expert_forward(): pl.pallas_call(forward_kernel, out_shape=(out(BF16), out(F32), out(F32)),...  142 us
    pallas_call x2, Pallas kernels, project(): pl.pallas_call(functools.partial(project_kernel, dims, len(acts)), out_sh...  132 us
    pallas_call x2, Pallas kernels, expert_backward(): pl.pallas_call(backward_kernel, out_shape=(out, out), grid_spec=pltpu.Pre...  132 us
    gather x2, local copies, waits for them, and re-layouts, pick_rows(): rows = jnp.take(back, jnp.maximum(pair_rows, 0), axis=0, mode='clip')  56.1 us
  transfers between devices with their start and end apart: 36, of which 12 were waited for; matrix products, arithmetic and copies ran while one was open for 9% of the time, Pallas kernels for 29%

profile of v2, /device:TPU:0, one launch (start us, length us, event | category | flops | bytes accessed | tf_op | source)
XLA Modules:
  0.0 1918.7 jit_solution(5335876553882405842)
XLA Ops:
  18.7 37.1 %all-gather.1 = f32[16,6,2048]{2,1,0:T(8,128)S(1)} all-gather(f32[1,6,2048]{2,1,0:T(8,128)S(1)} %bitcast.87), channel_id=2, replica_groups=mesh['etp'=2,'ep'=8] {'ep','etp'}, dimensions={0}, use_global_device_ids=true | all-gather | bytes 835584 | tf_op jit(solution)/shard_map/all_gather | solution.py:262
  64.6 7.5 constant_dynamic-slice_fusion.1
  78.4 182.7 %all-gather.7.cloned.1.call-done.rows_ref = bf16[32768,1024]{1,0:T(8,128)(2,1)} async-done(((bf16[2048,1024]{1,0:T(8,128)(2,1)}), bf16[32768,1024]{1,0:T(8,128)(2,1)}) %all-gather.7.cloned.1.call-update) | async-done | bytes 67108880 | tf_op jit(solution)/shard_map/all_gather | solution.py:247
  263.5 452.0 %all-gather.5.cloned.1.call-done.rows_ref = bf16[32768,1024]{1,0:T(8,128)(2,1)} async-done(((bf16[2048,1024]{1,0:T(8,128)(2,1)}), bf16[32768,1024]{1,0:T(8,128)(2,1)}) %all-gather.5.cloned.1.call-update) | async-done | bytes 67108880 | tf_op jit(solution)/shard_map/all_gather | solution.py:246
  715.4 83.4 %dispatch_x.1.x_ref = bf16[2,5120,1024]{2,1,0:T(8,128)(2,1)} custom-call(s32[2,65]{1,0:T(2,128)} %pad_add_fusion.start_ref, s32[2,32768]{1,0:T(2,128)} %bitcast.88, f32[2,32768]{1,0:T(2,128)} %fusion.6.gate_ref, bf16[32768,1024]{1,0:T(8,128)(2,1)} %all-gather.5.cloned.1.call-done.rows_ref), custom_call_target="tpu_custom_call" | custom-call | flops 40000000000 | bytes 90000000 | tf_op jit(solution)/shard_map/dispatch_x/pallas_call | solution.py:64
  799.4 94.3 %expert_forward.2 = (bf16[2,5120,1792]{2,1,0:T(8,128)(2,1)}, f32[2,5120,1792]{2,1,0:T(8,128)}, f32[2,5120,1792]{2,1,0:T(8,128)}) custom-call(s32[2]{0:T(128)} %iota.70.pick_ref, bf16[2,5120,1024]{2,1,0:T(8,128)(2,1)} %dispatch_x.1.x_ref, bf16[2,1024,1792]{2,1,0:T(8,128)(2,1)} %refs_4_.1, bf16[2,1024,1792]{2,1,0:T(8,128)(2,1)} %refs_5_.1), custom_call_target="tpu_custom_call" | custom-call | flops 75161927680 | bytes 220200960 | tf_op jit(solution)/shard_map/expert_forward/pallas_call | solution.py:102
  893.7 87.0 %dispatch_c.1.c_ref = bf16[2,5120,1024]{2,1,0:T(8,128)(2,1)} custom-call(s32[2,65]{1,0:T(2,128)} %pad_add_fusion.start_ref, s32[2,32768]{1,0:T(2,128)} %bitcast.89, f32[2,32768]{1,0:T(2,128)} %fusion.6.gate_ref, bf16[32768,1024]{1,0:T(8,128)(2,1)} %all-gather.7.cloned.1.call-done.rows_ref), custom_call_target="tpu_custom_call" | custom-call | flops 40000000000 | bytes 90000000 | tf_op jit(solution)/shard_map/dispatch_c/pallas_call | solution.py:64
  981.1 86.6 %expert_backward.2 = (bf16[2,5120,1792]{2,1,0:T(8,128)(2,1)}, bf16[2,5120,1792]{2,1,0:T(8,128)(2,1)}) custom-call(s32[2]{0:T(128)} %iota.74.pick_ref, bf16[2,5120,1024]{2,1,0:T(8,128)(2,1)} %dispatch_c.1.c_ref, bf16[2,1792,1024]{2,1,0:T(8,128)(2,1)} %refs_2_.1, f32[2,5120,1792]{2,1,0:T(8,128)} %get-tuple-element.108.s_ref, ...), custom_call_target="tpu_custom_call" | custom-call | flops 37580963840 | bytes 220200960 | tf_op jit(solution)/shard_map/expert_backward/pallas_call | solution.py:131
  1067.7 47.6 %expert_forward.3 = (bf16[1,5120,1792]{2,1,0:T(8,128)(2,1)}, f32[1,5120,1792]{2,1,0:T(8,128)}, f32[1,5120,1792]{2,1,0:T(8,128)}) custom-call(s32[1]{0:T(128)} %bitcast.16.pick_ref, bf16[2,5120,1024]{2,1,0:T(8,128)(2,1)} %dispatch_x.1.x_ref, bf16[1,1024,1792]{2,1,0:T(8,128)(2,1)} %collective-permute-done.wg_ref.refs_6_, ...), custom_call_target="tpu_custom_call" | custom-call | flops 37580963840 | bytes 110100480 | tf_op jit(solution)/shard_map/expert_forward/pallas_call | solution.py:102
  1115.4 45.1 %shard_map.126.rows_ref = bf16[5120,1024]{1,0:T(8,128)(2,1)} custom-call(s32[1]{0:T(128)} %bitcast.16.pick_ref, bf16[2,5120,1792]{2,1,0:T(8,128)(2,1)} %get-tuple-element.194.refs_0_, bf16[1,5120,1792]{2,1,0:T(8,128)(2,1)} %get-tuple-element.115.refs_1_, bf16[2,1792,1024]{2,1,0:T(8,128)(2,1)} %refs_2_.1, ...), custom_call_target="tpu_custom_call" | custom-call | flops 37580963840 | bytes 36700160 | tf_op jit(solution)/shard_map/pallas_call | solution.py:169
  1160.5 10.2 cut_windows.2
  1174.5 45.0 %expert_backward.3 = (bf16[1,5120,1792]{2,1,0:T(8,128)(2,1)}, bf16[1,5120,1792]{2,1,0:T(8,128)(2,1)}) custom-call(s32[1]{0:T(128)} %bitcast.16.pick_ref, bf16[2,5120,1024]{2,1,0:T(8,128)(2,1)} %dispatch_c.1.c_ref, bf16[1,1792,1024]{2,1,0:T(8,128)(2,1)} %collective-permute-done.2.refs_3_.wd_ref, f32[1,5120,1792]{2,1,0:T(8,128)} %get-tuple-element.152.s_ref, ...), custom_call_target="tpu_custom_call" | custom-call | flops 18790481920 | bytes 110100480 | tf_op jit(solution)/shard_map/expert_backward/pallas_call | solution.py:131
  1219.5 87.0 %shard_map.127.rows_ref = bf16[5120,1024]{1,0:T(8,128)(2,1)} custom-call(s32[1]{0:T(128)} %bitcast.16.pick_ref, bf16[2,5120,1792]{2,1,0:T(8,128)(2,1)} %get-tuple-element.192.refs_0_, bf16[2,5120,1792]{2,1,0:T(8,128)(2,1)} %get-tuple-element.193.refs_1_, bf16[1,5120,1792]{2,1,0:T(8,128)(2,1)} %get-tuple-element.154.refs_2_, ...), custom_call_target="tpu_custom_call" | custom-call | flops 75161927680 | bytes 73400320 | tf_op jit(solution)/shard_map/pallas_call | solution.py:169
  1306.5 10.3 cut_windows.3
  1323.6 47.5 %fusion.30 = f32[2,1024,1792]{2,1,0:T(8,128)} fusion(bf16[2,5120,1024]{2,1,0:T(8,128)(2,1)} %dispatch_x.1.x_ref, bf16[2,5120,1792]{2,1,0:T(8,128)(2,1)} %get-tuple-element.192.refs_0_), kind=kOutput, calls=%fused_computation.99 | convolution fusion | flops 37580963840 | bytes 72351744 | tf_op jit(solution)/shard_map/erd,erf->edf/dot_general | solution.py:324
  1373.0 6.9 collective-permute-done.9.refs_7_
  1384.4 79.8 %collective-permute-done.12.refs_10_ = bf16[464,1024]{1,0:T(8,128)(2,1)} collective-permute-done((bf16[464,1024]{1,0:T(8,128)(2,1)}, bf16[464,1024]{1,0:T(8,128)(2,1)}, u32[]{:S(2)}, u32[]{:S(2)}) %collective-permute-start.12) | collective-permute-done | bytes 950304 | tf_op jit(solution)/shard_map/ppermute | solution.py:310
  1466.3 47.7 %fusion.31 = f32[2,1024,1792]{2,1,0:T(8,128)} fusion(bf16[2,5120,1024]{2,1,0:T(8,128)(2,1)} %dispatch_x.1.x_ref, bf16[2,5120,1792]{2,1,0:T(8,128)(2,1)} %get-tuple-element.193.refs_1_), kind=kOutput, calls=%fused_computation.100 | convolution fusion | flops 37580963840 | bytes 72351744 | tf_op jit(solution)/shard_map/erd,erf->edf/dot_general | solution.py:325
  1518.8 11.1 join_windows.2
  1529.8 28.1 %gather_fusion.1 = bf16[4096,1024]{1,0:T(8,128)(2,1)} fusion(bf16[7424,1024]{1,0:T(8,128)(2,1)} %join_windows.2, s32[4096]{0:T(1024)S(1)} %copy-done.19), kind=kCustom, calls=%fused_computation.1 | custom fusion | bytes 16793600 | tf_op jit(solution)/shard_map/jit(_take)/gather | solution.py:336
  1565.4 5.4 copy-done.1
  1579.5 14.3 collective-permute-done.23.refs_6_
  1594.3 34.9 %collective-permute-done.24.refs_7_ = bf16[464,1024]{1,0:T(8,128)(2,1)} collective-permute-done((bf16[464,1024]{1,0:T(8,128)(2,1)}, bf16[464,1024]{1,0:T(8,128)(2,1)}, u32[]{:S(2)}, u32[]{:S(2)}) %collective-permute-start.24) | collective-permute-done | bytes 950304 | tf_op jit(solution)/shard_map/ppermute | solution.py:310
  1631.7 44.4 %collective-permute-done.26.refs_9_ = bf16[464,1024]{1,0:T(8,128)(2,1)} collective-permute-done((bf16[464,1024]{1,0:T(8,128)(2,1)}, bf16[464,1024]{1,0:T(8,128)(2,1)}, u32[]{:S(2)}, u32[]{:S(2)}) %collective-permute-start.26) | collective-permute-done | bytes 950304 | tf_op jit(solution)/shard_map/ppermute | solution.py:310
  1676.1 40.8 %collective-permute-done.27.refs_10_ = bf16[464,1024]{1,0:T(8,128)(2,1)} collective-permute-done((bf16[464,1024]{1,0:T(8,128)(2,1)S(1)}, bf16[464,1024]{1,0:T(8,128)(2,1)}, u32[]{:S(2)}, u32[]{:S(2)}) %collective-permute-start.27) | collective-permute-done | bytes 950304 | tf_op jit(solution)/shard_map/ppermute | solution.py:310
  1719.4 10.1 add_convert_fusion
  1729.5 27.9 %collective-permute-done.28.refs_11_ = bf16[464,1024]{1,0:T(8,128)(2,1)S(1)} collective-permute-done((bf16[464,1024]{1,0:T(8,128)(2,1)}, bf16[464,1024]{1,0:T(8,128)(2,1)S(1)}, u32[]{:S(2)}, u32[]{:S(2)}) %collective-permute-start.28) | collective-permute-done | bytes 950304 | tf_op jit(solution)/shard_map/ppermute | solution.py:310
  1758.4 10.9 join_windows.3
  1769.3 28.1 %gather_fusion.2 = bf16[4096,1024]{1,0:T(8,128)(2,1)} fusion(bf16[7424,1024]{1,0:T(8,128)(2,1)} %join_windows.3, s32[4096]{0:T(1024)S(1)} %copy-done.20), kind=kCustom, calls=%fused_computation.2 | custom fusion | bytes 16793600 | tf_op jit(solution)/shard_map/jit(_take)/gather | solution.py:336
  1797.4 49.4 %fusion.32 = f32[2,1792,1024]{2,1,0:T(8,128)} fusion(bf16[2,5120,1792]{2,1,0:T(8,128)(2,1)} %get-tuple-element.194.refs_0_, bf16[2,5120,1024]{2,1,0:T(8,128)(2,1)} %dispatch_c.1.c_ref), kind=kOutput, calls=%fused_computation.101 | convolution fusion | flops 37580963840 | bytes 72351744 | tf_op jit(solution)/shard_map/erf,erd->efd/dot_general | solution.py:356
  1846.8 5.0 convert_select_fusion
  1855.0 54.3 %all-reduce.4.cloned.1.call-done = f32[1024,16]{0,1:T(8,128)} async-done(((f32[1024,16]{0,1:T(8,128)}), f32[1024,16]{0,1:T(8,128)}) %all-reduce.4.cloned.1.call-update) | async-done | bytes 65552 | tf_op jit(solution)/shard_map/psum | solution.py:355
  (196 shorter events, 80.0 us)
Async XLA Ops:
  7.2 253.9 %all-gather.7.cloned.1.call-start = ((), (), s32[]{:S(2)}) async-start(), calls=%async_computation.1 | async-start | bytes 71303168 | tf_op jit(solution)/shard_map/all_gather | solution.py:247
  7.9 707.5 %all-gather.5.cloned.1.call-start = ((), (), s32[]{:S(2)}) async-start(), calls=%async_computation | async-start | bytes 71303168 | tf_op jit(solution)/shard_map/all_gather | solution.py:246
  8.7 1900.6 %all-reduce.4.cloned.1.call-start = ((), (), s32[]{:S(2)}) async-start(), calls=%async_computation.2 | async-start | bytes 131072 | tf_op jit(solution)/shard_map/psum | solution.py:355
  261.1 806.6 %collective-permute-start = (bf16[1,1024,1792]{2,1,0:T(8,128)(2,1)}, bf16[1,1024,1792]{2,1,0:T(8,128)(2,1)}, u32[]{:S(2)}, u32[]{:S(2)}) collective-permute-start(bf16[1,1024,1792]{2,1,0:T(8,128)(2,1)} %get-tuple-element.113), channel_id=1, source_target_pairs={{0,8},{8,0},{1,9},{9,1},{2,10},{10,2},{3,11},{11,3},{4,12},{12,4},... | collective-permute-start | bytes 11010056 | tf_op jit(solution)/shard_map/ppermute | solution.py:294
  261.5 806.3 %collective-permute-start.1 = (bf16[1,1024,1792]{2,1,0:T(8,128)(2,1)}, bf16[1,1024,1792]{2,1,0:T(8,128)(2,1)}, u32[]{:S(2)}, u32[]{:S(2)}) collective-permute-start(bf16[1,1024,1792]{2,1,0:T(8,128)(2,1)} %get-tuple-element.114), channel_id=1, source_target_pairs={{0,8},{8,0},{1,9},{9,1},{2,10},{10,2},{3,11},{11,3},{4,12},{12,4},... | collective-permute-start | bytes 11010056 | tf_op jit(solution)/shard_map/ppermute | solution.py:294
  263.1 852.2 %collective-permute-start.2 = (bf16[1,1792,1024]{2,1,0:T(8,128)(2,1)}, bf16[1,1792,1024]{2,1,0:T(8,128)(2,1)}, u32[]{:S(2)}, u32[]{:S(2)}) collective-permute-start(bf16[1,1792,1024]{2,1,0:T(8,128)(2,1)} %constant_dynamic-slice_fusion), channel_id=1, source_target_pairs={{0,8},{8,0},{1,9},{9,1},{2,10},{10,2},{3,11},{11,3},{4,12},{12,4},... | collective-permute-start | bytes 11010056 | tf_op jit(solution)/shard_map/ppermute | solution.py:294
  1170.7 146.2 %collective-permute-start.3 = (bf16[464,1024]{1,0:T(8,128)(2,1)}, bf16[464,1024]{1,0:T(8,128)(2,1)S(1)}, u32[]{:S(2)}, u32[]{:S(2)}) collective-permute-start(bf16[464,1024]{1,0:T(8,128)(2,1)} %get-tuple-element.135), channel_id=1, source_target_pairs={{0,8},{8,0},{1,9},{9,1},{2,10},{10,2},{3,11},{11,3},{4,12},{12,4},... | collective-permute-start | bytes 2850824 | tf_op jit(solution)/shard_map/ppermute | solution.py:310
  1170.9 146.0 %collective-permute-start.4 = (bf16[464,1024]{1,0:T(8,128)(2,1)}, bf16[464,1024]{1,0:T(8,128)(2,1)S(1)}, u32[]{:S(2)}, u32[]{:S(2)}) collective-permute-start(bf16[464,1024]{1,0:T(8,128)(2,1)} %get-tuple-element.136), channel_id=1, source_target_pairs={{0,1},{8,9},{1,0},{9,8},{2,3},{10,11},{3,2},{11,10},{4,5},{12,13},... | collective-permute-start | bytes 2850824 | tf_op jit(solution)/shard_map/ppermute | solution.py:310
  1170.9 149.1 %collective-permute-start.5 = (bf16[464,1024]{1,0:T(8,128)(2,1)}, bf16[464,1024]{1,0:T(8,128)(2,1)}, u32[]{:S(2)}, u32[]{:S(2)}) collective-permute-start(bf16[464,1024]{1,0:T(8,128)(2,1)} %get-tuple-element.137), channel_id=1, source_target_pairs={{0,9},{8,1},{1,8},{9,0},{2,11},{10,3},{3,10},{11,2},{4,13},{12,5},... | collective-permute-start | bytes 2850824 | tf_op jit(solution)/shard_map/ppermute | solution.py:310
  1172.8 149.9 %collective-permute-start.6 = (bf16[464,1024]{1,0:T(8,128)(2,1)}, bf16[464,1024]{1,0:T(8,128)(2,1)}, u32[]{:S(2)}, u32[]{:S(2)}) collective-permute-start(bf16[464,1024]{1,0:T(8,128)(2,1)} %get-tuple-element.138), channel_id=1, source_target_pairs={{0,2},{8,10},{1,3},{9,11},{2,0},{10,8},{3,1},{11,9},{4,6},{12,14},... | collective-permute-start | bytes 2850824 | tf_op jit(solution)/shard_map/ppermute | solution.py:310
  1172.8 149.9 %collective-permute-start.7 = (bf16[464,1024]{1,0:T(8,128)(2,1)}, bf16[464,1024]{1,0:T(8,128)(2,1)}, u32[]{:S(2)}, u32[]{:S(2)}) collective-permute-start(bf16[464,1024]{1,0:T(8,128)(2,1)} %get-tuple-element.139), channel_id=1, source_target_pairs={{0,10},{8,2},{1,11},{9,3},{2,8},{10,0},{3,9},{11,1},{4,14},{12,6},... | collective-permute-start | bytes 2850824 | tf_op jit(solution)/shard_map/ppermute | solution.py:310
  1316.9 54.2 %collective-permute-start.8 = (bf16[464,1024]{1,0:T(8,128)(2,1)}, bf16[464,1024]{1,0:T(8,128)(2,1)S(1)}, u32[]{:S(2)}, u32[]{:S(2)}) collective-permute-start(bf16[464,1024]{1,0:T(8,128)(2,1)} %get-tuple-element.140), channel_id=1, source_target_pairs={{0,3},{8,11},{1,2},{9,10},{2,1},{10,9},{3,0},{11,8},{4,7},{12,15},... | collective-permute-start | bytes 2850824 | tf_op jit(solution)/shard_map/ppermute | solution.py:310
  1317.0 63.0 %collective-permute-start.9 = (bf16[464,1024]{1,0:T(8,128)(2,1)}, bf16[464,1024]{1,0:T(8,128)(2,1)}, u32[]{:S(2)}, u32[]{:S(2)}) collective-permute-start(bf16[464,1024]{1,0:T(8,128)(2,1)} %get-tuple-element.141), channel_id=1, source_target_pairs={{0,11},{8,3},{1,10},{9,2},{2,9},{10,1},{3,8},{11,0},{4,15},{12,7},... | collective-permute-start | bytes 2850824 | tf_op jit(solution)/shard_map/ppermute | solution.py:310
  1320.0 61.9 %collective-permute-start.10 = (bf16[464,1024]{1,0:T(8,128)(2,1)}, bf16[464,1024]{1,0:T(8,128)(2,1)}, u32[]{:S(2)}, u32[]{:S(2)}) collective-permute-start(bf16[464,1024]{1,0:T(8,128)(2,1)} %get-tuple-element.142), channel_id=1, source_target_pairs={{0,4},{8,12},{1,5},{9,13},{2,6},{10,14},{3,7},{11,15},{4,0},{12,8}... | collective-permute-start | bytes 2850824 | tf_op jit(solution)/shard_map/ppermute | solution.py:310
  1322.7 60.2 %collective-permute-start.11 = (bf16[464,1024]{1,0:T(8,128)(2,1)}, bf16[464,1024]{1,0:T(8,128)(2,1)}, u32[]{:S(2)}, u32[]{:S(2)}) collective-permute-start(bf16[464,1024]{1,0:T(8,128)(2,1)} %get-tuple-element.143), channel_id=1, source_target_pairs={{0,12},{8,4},{1,13},{9,5},{2,14},{10,6},{3,15},{11,7},{4,8},{12,0}... | collective-permute-start | bytes 2850824 | tf_op jit(solution)/shard_map/ppermute | solution.py:310
  1322.7 141.5 %collective-permute-start.12 = (bf16[464,1024]{1,0:T(8,128)(2,1)}, bf16[464,1024]{1,0:T(8,128)(2,1)}, u32[]{:S(2)}, u32[]{:S(2)}) collective-permute-start(bf16[464,1024]{1,0:T(8,128)(2,1)} %get-tuple-element.144), channel_id=1, source_target_pairs={{0,5},{8,13},{1,4},{9,12},{2,7},{10,15},{3,6},{11,14},{4,1},{12,9}... | collective-permute-start | bytes 2850824 | tf_op jit(solution)/shard_map/ppermute | solution.py:310
  1371.1 142.9 %collective-permute-start.13 = (bf16[464,1024]{1,0:T(8,128)(2,1)}, bf16[464,1024]{1,0:T(8,128)(2,1)}, u32[]{:S(2)}, u32[]{:S(2)}) collective-permute-start(bf16[464,1024]{1,0:T(8,128)(2,1)} %get-tuple-element.145), channel_id=1, source_target_pairs={{0,13},{8,5},{1,12},{9,4},{2,15},{10,7},{3,14},{11,6},{4,9},{12,1}... | collective-permute-start | bytes 2850824 | tf_op jit(solution)/shard_map/ppermute | solution.py:310
  1379.9 134.4 %collective-permute-start.14 = (bf16[464,1024]{1,0:T(8,128)(2,1)}, bf16[464,1024]{1,0:T(8,128)(2,1)}, u32[]{:S(2)}, u32[]{:S(2)}) collective-permute-start(bf16[464,1024]{1,0:T(8,128)(2,1)} %get-tuple-element.146), channel_id=1, source_target_pairs={{0,6},{8,14},{1,7},{9,15},{2,4},{10,12},{3,5},{11,13},{4,2},{12,10... | collective-permute-start | bytes 2850824 | tf_op jit(solution)/shard_map/ppermute | solution.py:310
  1381.9 132.4 %collective-permute-start.15 = (bf16[464,1024]{1,0:T(8,128)(2,1)}, bf16[464,1024]{1,0:T(8,128)(2,1)}, u32[]{:S(2)}, u32[]{:S(2)}) collective-permute-start(bf16[464,1024]{1,0:T(8,128)(2,1)} %get-tuple-element.147), channel_id=1, source_target_pairs={{0,14},{8,6},{1,15},{9,7},{2,12},{10,4},{3,13},{11,5},{4,10},{12,2... | collective-permute-start | bytes 2850824 | tf_op jit(solution)/shard_map/ppermute | solution.py:310
  1383.0 133.3 %collective-permute-start.16 = (bf16[464,1024]{1,0:T(8,128)(2,1)}, bf16[464,1024]{1,0:T(8,128)(2,1)}, u32[]{:S(2)}, u32[]{:S(2)}) collective-permute-start(bf16[464,1024]{1,0:T(8,128)(2,1)} %get-tuple-element.148), channel_id=1, source_target_pairs={{0,7},{8,15},{1,6},{9,14},{2,5},{10,13},{3,4},{11,12},{4,3},{12,11... | collective-permute-start | bytes 2850824 | tf_op jit(solution)/shard_map/ppermute | solution.py:310
  1514.0 56.7 %collective-permute-start.18 = (bf16[464,1024]{1,0:T(8,128)(2,1)}, bf16[464,1024]{1,0:T(8,128)(2,1)S(1)}, u32[]{:S(2)}, u32[]{:S(2)}) collective-permute-start(bf16[464,1024]{1,0:T(8,128)(2,1)} %get-tuple-element.173), channel_id=1, source_target_pairs={{0,8},{8,0},{1,9},{9,1},{2,10},{10,2},{3,11},{11,3},{4,12},{12,4},... | collective-permute-start | bytes 2850824 | tf_op jit(solution)/shard_map/ppermute | solution.py:310
  1514.3 57.6 %collective-permute-start.19 = (bf16[464,1024]{1,0:T(8,128)(2,1)}, bf16[464,1024]{1,0:T(8,128)(2,1)S(1)}, u32[]{:S(2)}, u32[]{:S(2)}) collective-permute-start(bf16[464,1024]{1,0:T(8,128)(2,1)} %get-tuple-element.174), channel_id=1, source_target_pairs={{0,1},{8,9},{1,0},{9,8},{2,3},{10,11},{3,2},{11,10},{4,5},{12,13},... | collective-permute-start | bytes 2850824 | tf_op jit(solution)/shard_map/ppermute | solution.py:310
  1514.3 61.9 %collective-permute-start.20 = (bf16[464,1024]{1,0:T(8,128)(2,1)}, bf16[464,1024]{1,0:T(8,128)(2,1)}, u32[]{:S(2)}, u32[]{:S(2)}) collective-permute-start(bf16[464,1024]{1,0:T(8,128)(2,1)} %get-tuple-element.175), channel_id=1, source_target_pairs={{0,9},{8,1},{1,8},{9,0},{2,11},{10,3},{3,10},{11,2},{4,13},{12,5},... | collective-permute-start | bytes 2850824 | tf_op jit(solution)/shard_map/ppermute | solution.py:310
  1516.2 61.8 %collective-permute-start.21 = (bf16[464,1024]{1,0:T(8,128)(2,1)}, bf16[464,1024]{1,0:T(8,128)(2,1)}, u32[]{:S(2)}, u32[]{:S(2)}) collective-permute-start(bf16[464,1024]{1,0:T(8,128)(2,1)} %get-tuple-element.176), channel_id=1, source_target_pairs={{0,2},{8,10},{1,3},{9,11},{2,0},{10,8},{3,1},{11,9},{4,6},{12,14},... | collective-permute-start | bytes 2850824 | tf_op jit(solution)/shard_map/ppermute | solution.py:310
  1517.7 60.9 %collective-permute-start.22 = (bf16[464,1024]{1,0:T(8,128)(2,1)}, bf16[464,1024]{1,0:T(8,128)(2,1)}, u32[]{:S(2)}, u32[]{:S(2)}) collective-permute-start(bf16[464,1024]{1,0:T(8,128)(2,1)} %get-tuple-element.177), channel_id=1, source_target_pairs={{0,10},{8,2},{1,11},{9,3},{2,8},{10,0},{3,9},{11,1},{4,14},{12,6},... | collective-permute-start | bytes 2850824 | tf_op jit(solution)/shard_map/ppermute | solution.py:310
  1571.9 57.2 %collective-permute-start.24 = (bf16[464,1024]{1,0:T(8,128)(2,1)}, bf16[464,1024]{1,0:T(8,128)(2,1)}, u32[]{:S(2)}, u32[]{:S(2)}) collective-permute-start(bf16[464,1024]{1,0:T(8,128)(2,1)} %get-tuple-element.179), channel_id=1, source_target_pairs={{0,11},{8,3},{1,10},{9,2},{2,9},{10,1},{3,8},{11,0},{4,15},{12,7},... | collective-permute-start | bytes 2850824 | tf_op jit(solution)/shard_map/ppermute | solution.py:310
  1578.1 98.0 %collective-permute-start.26 = (bf16[464,1024]{1,0:T(8,128)(2,1)}, bf16[464,1024]{1,0:T(8,128)(2,1)}, u32[]{:S(2)}, u32[]{:S(2)}) collective-permute-start(bf16[464,1024]{1,0:T(8,128)(2,1)} %get-tuple-element.181), channel_id=1, source_target_pairs={{0,12},{8,4},{1,13},{9,5},{2,14},{10,6},{3,15},{11,7},{4,8},{12,0}... | collective-permute-start | bytes 2850824 | tf_op jit(solution)/shard_map/ppermute | solution.py:310
  1578.7 138.3 %collective-permute-start.27 = (bf16[464,1024]{1,0:T(8,128)(2,1)S(1)}, bf16[464,1024]{1,0:T(8,128)(2,1)}, u32[]{:S(2)}, u32[]{:S(2)}) collective-permute-start(bf16[464,1024]{1,0:T(8,128)(2,1)S(1)} %copy-done.31), channel_id=1, source_target_pairs={{0,5},{8,13},{1,4},{9,12},{2,7},{10,15},{3,6},{11,14},{4,1},{12,9}... | collective-permute-start | bytes 2850824 | tf_op jit(solution)/shard_map/ppermute | solution.py:310
  1593.7 163.7 %collective-permute-start.28 = (bf16[464,1024]{1,0:T(8,128)(2,1)}, bf16[464,1024]{1,0:T(8,128)(2,1)S(1)}, u32[]{:S(2)}, u32[]{:S(2)}) collective-permute-start(bf16[464,1024]{1,0:T(8,128)(2,1)} %get-tuple-element.183), channel_id=1, source_target_pairs={{0,13},{8,5},{1,12},{9,4},{2,15},{10,7},{3,14},{11,6},{4,9},{12,1}... | collective-permute-start | bytes 2850824 | tf_op jit(solution)/shard_map/ppermute | solution.py:310
  1629.1 129.2 %collective-permute-start.29 = (bf16[464,1024]{1,0:T(8,128)(2,1)}, bf16[464,1024]{1,0:T(8,128)(2,1)}, u32[]{:S(2)}, u32[]{:S(2)}) collective-permute-start(bf16[464,1024]{1,0:T(8,128)(2,1)} %get-tuple-element.184), channel_id=1, source_target_pairs={{0,6},{8,14},{1,7},{9,15},{2,4},{10,12},{3,5},{11,13},{4,2},{12,10... | collective-permute-start | bytes 2850824 | tf_op jit(solution)/shard_map/ppermute | solution.py:310
  1629.1 129.2 %collective-permute-start.30 = (bf16[464,1024]{1,0:T(8,128)(2,1)}, bf16[464,1024]{1,0:T(8,128)(2,1)}, u32[]{:S(2)}, u32[]{:S(2)}) collective-permute-start(bf16[464,1024]{1,0:T(8,128)(2,1)} %get-tuple-element.185), channel_id=1, source_target_pairs={{0,14},{8,6},{1,15},{9,7},{2,12},{10,4},{3,13},{11,5},{4,10},{12,2... | collective-permute-start | bytes 2850824 | tf_op jit(solution)/shard_map/ppermute | solution.py:310
  1676.1 82.2 %collective-permute-start.31 = (bf16[464,1024]{1,0:T(8,128)(2,1)}, bf16[464,1024]{1,0:T(8,128)(2,1)}, u32[]{:S(2)}, u32[]{:S(2)}) collective-permute-start(bf16[464,1024]{1,0:T(8,128)(2,1)} %get-tuple-element.186), channel_id=1, source_target_pairs={{0,7},{8,15},{1,6},{9,14},{2,5},{10,13},{3,4},{11,12},{4,3},{12,11... | collective-permute-start | bytes 2850824 | tf_op jit(solution)/shard_map/ppermute | solution.py:310
  (37 other events, 1315.4 us)
Sparse Core Ops, SparseCore 0:
  10.2 250.8 all-gather.6
  263.3 452.0 all-gather.4
  1846.9 62.3 all-reduce.3
